TPU v7x, 32 devices: a whole 2x2x4 slice. The times are simulated.
32 devices in a mesh: gx: 2 (over x), gy: 4 (over y, core), gz: 4 (over z).
Axes of the slice: x: 2, y: 2, z: 4, core: 2. Of those that a mesh axis runs over, the one named last changes fastest.
Arguments:
- displacement: float32 [3, 16, 32, 512], P(None, 'gx', 'gz', 'gy'), may hold values from -0.1 to 0.1
- velocity: float32 [3, 16, 32, 512], P(None, 'gx', 'gz', 'gy'), may hold values from -0.4 to 0.4
- body_force: float32 [3, 16, 32, 512], P(None, 'gx', 'gz', 'gy'), may hold values from -4 to 4
- broken: int32 [12, 16, 32, 512], P(None, 'gx', 'gz', 'gy'), may hold values from 0 to 1073741823
Outputs:
- new_displacement: float32 [3, 16, 32, 512], P(None, 'gx', 'gz', 'gy')
- new_velocity: float32 [3, 16, 32, 512], P(None, 'gx', 'gz', 'gy')
- new_acceleration: float32 [3, 16, 32, 512], P(None, 'gx', 'gz', 'gy')
- strain_energy: float32 [], replicated
All inputs are finite; a program needn't handle non-finite values.
Results may differ from a plain program's by a relative error of at most 0.0003.
Values sent between devices are 32-bit elements; how exact they have to be, the bound alone decides.
A program may use at most 128 MiB of HBM per device.

v0:
```python
import functools
import math

import jax
import jax.numpy as jnp
from jax import lax
from jax.experimental import pallas as pl
from jax.experimental.pallas import tpu as pltpu
from jax.sharding import PartitionSpec as P

TIME_STEP = 0.05
MICRO_MODULUS = 4.0
BITS_PER_WORD = 30
W = 3
REACH = range(-W, W + 1)
BONDS = tuple(
    (p, q, r) for p in REACH for q in REACH for r in REACH if (p, q, r) != (0, 0, 0)
)
INDEX = {bond: k for k, bond in enumerate(BONDS)}
WORD_COUNT = -(-len(BONDS) // BITS_PER_WORD)


def extended(block, axis, dim):
    count = lax.axis_size(axis)
    forward = [(i, (i + 1) % count) for i in range(count)]
    backward = [(t, s) for s, t in forward]
    low = lax.ppermute(
        lax.slice_in_dim(block, block.shape[dim] - W, None, axis=dim), axis, forward
    )
    high = lax.ppermute(lax.slice_in_dim(block, 0, W, axis=dim), axis, backward)
    return low, high


def depth_bits(shape, depth_start, depth_total):
    depth = lax.broadcasted_iota(jnp.int32, shape, 0) + depth_start
    words = [jnp.zeros(shape, jnp.int32) for _ in range(WORD_COUNT)]
    for q in REACH:
        if q == 0:
            continue
        outside = (depth + q < 0) | (depth + q >= depth_total)
        for w in range(WORD_COUNT):
            bits = 0
            for (p, q2, r), k in INDEX.items():
                if q2 == q and k // BITS_PER_WORD == w:
                    bits |= 1 << (k % BITS_PER_WORD)
            if bits:
                words[w] = words[w] | jnp.where(outside, bits, 0)
    return words


def store_masks(broken_ref, mask_ref, outside_ref, depth_start, depth_total):
    rows = broken_ref.shape[1]
    for w, word in enumerate(depth_bits(broken_ref.shape[2:], depth_start, depth_total)):
        outside_ref[w] = word

    def body(x, carry):
        for w in range(WORD_COUNT):
            word = broken_ref[w, x] | outside_ref[w]
            for k in range(w * BITS_PER_WORD, min(len(BONDS), (w + 1) * BITS_PER_WORD)):
                p, q, r = BONDS[k]
                weight = MICRO_MODULUS * math.exp(-(p * p + q * q + r * r) / 9.0)
                bit = word & (1 << (k % BITS_PER_WORD))
                mask_ref[k, x] = jnp.where(bit == 0, jnp.float32(weight), jnp.float32(0.0))
        return carry

    lax.fori_loop(0, rows, body, 0)


def shifted_rows(a, b, lane, e_ref, c, x):
    width = a.shape[1]
    depth = a.shape[0]
    for r in REACH:
        if r == 0:
            tile = a
        elif r > 0:
            tile = pltpu.roll(jnp.where(lane < r, b, a), width - r, 1)
        else:
            tile = pltpu.roll(jnp.where(lane >= width + r, b, a), -r, 1)
        if c == 2 and r != 0:
            tile = tile + float(r)
        e_ref[r + W, c, x, 0:depth] = tile


def bond_rows(x, steps, e_ref, mask_ref, depth, with_energy):
    center = [e_ref[W, c, x + W, W : W + depth] for c in range(3)]
    force = [jnp.zeros_like(center[0]) for _ in range(3)]
    energy = jnp.zeros_like(center[0])
    for p in steps:
        center_x = center[0] - float(p)
        for q in REACH:
            center_z = center[1] - float(q)
            for r in REACH:
                if (p, q, r) == (0, 0, 0):
                    continue
                k = INDEX[(p, q, r)]
                rest = math.sqrt(p * p + q * q + r * r)
                nb = [
                    e_ref[r + W, c, x + (W + p), W + q : W + q + depth] for c in range(3)
                ]
                bx = nb[0] - center_x
                bz = nb[1] - center_z
                by = nb[2] - center[2]
                square = bx * bx + bz * bz + by * by
                h = jnp.float32(1.0 / rest) - lax.rsqrt(square)
                g = mask_ref[k, x] * h
                force[0] = force[0] + g * bx
                force[1] = force[1] + g * bz
                force[2] = force[2] + g * by
                if with_energy:
                    energy = energy + (g * jnp.float32(0.25 * rest)) * (h * square)
    return force, energy


def pass_kernel(
    depth_total, with_energy, a_ref, b_ref, broken_ref, force_ref, energy_ref,
    e_ref, mask_ref, outside_ref,
):
    rows, depth = broken_ref.shape[1], broken_ref.shape[2]
    width = a_ref.shape[3]
    depth_start = lax.axis_index("gz") * depth
    store_masks(broken_ref, mask_ref, outside_ref, depth_start, depth_total)
    lane = lax.broadcasted_iota(jnp.int32, a_ref.shape[2:], 1)

    def fill(x, carry):
        for c in range(3):
            shifted_rows(a_ref[c, x], b_ref[c, x], lane, e_ref, c, x)
        return carry

    lax.fori_loop(0, rows + 2 * W, fill, 0)
    energy_ref[...] = jnp.zeros_like(energy_ref)

    def body(x, carry):
        force, energy = bond_rows(x, REACH, e_ref, mask_ref, depth, with_energy)
        for c in range(3):
            force_ref[c, x] = force[c]
        if with_energy:
            energy_ref[...] += energy
        return carry

    lax.fori_loop(0, rows, body, 0)


def bond_sum(field, broken, with_energy):
    _, rows, depth, width = field.shape
    depth_total = depth * lax.axis_size("gz")
    low, high = extended(field, "gx", 1)
    field = jnp.concatenate([low, field, high], axis=1)
    low, high = extended(field, "gz", 2)
    field = jnp.concatenate([low, field, high], axis=2)
    low, high = extended(field, "gy", 3)
    sides = jnp.concatenate(
        [high, jnp.zeros(field.shape[:3] + (width - 2 * W,), field.dtype), low], axis=3
    )
    padded = -(-(depth + 2 * W) // 8) * 8
    return pl.pallas_call(
        functools.partial(pass_kernel, depth_total, with_energy),
        out_shape=(
            jax.ShapeDtypeStruct((3, rows, depth, width), jnp.float32),
            jax.ShapeDtypeStruct((depth, width), jnp.float32),
        ),
        in_specs=[pl.BlockSpec(memory_space=pltpu.VMEM)] * 3,
        out_specs=(pl.BlockSpec(memory_space=pltpu.VMEM),) * 2,
        scratch_shapes=[
            pltpu.VMEM((2 * W + 1, 3, rows + 2 * W, padded, width), jnp.float32),
            pltpu.VMEM((len(BONDS), rows, depth, width), jnp.float32),
            pltpu.VMEM((WORD_COUNT, depth, width), jnp.int32),
        ],
        compiler_params=pltpu.CompilerParams(vmem_limit_bytes=48 * 1024 * 1024),
    )(field, sides, broken)


AXES = ("gx", "gy", "gz")


def sum_kernel(counts, tile_ref, total_ref, *scratch):
    slots, (send_sem, recv_sem) = scratch[: len(AXES)], scratch[len(AXES) :]
    barrier = pltpu.get_barrier_semaphore()
    peers = 0
    for axis, count in zip(AXES, counts):
        me = lax.axis_index(axis)
        for d in range(1, count):
            pl.semaphore_signal(
                barrier,
                inc=1,
                device_id={axis: lax.rem(me + d, count)},
                device_id_type=pl.DeviceIdType.MESH,
            )
            peers += 1
    pl.semaphore_wait(barrier, peers)
    at = 0
    value = tile_ref[...]
    for slot, axis, count in zip(slots, AXES, counts):
        me = lax.axis_index(axis)
        slot[me] = value
        copies = []
        for d in range(1, count):
            copy = pltpu.make_async_remote_copy(
                src_ref=slot.at[me],
                dst_ref=slot.at[me],
                send_sem=send_sem.at[at],
                recv_sem=recv_sem.at[at],
                device_id={axis: lax.rem(me + d, count)},
                device_id_type=pl.DeviceIdType.MESH,
            )
            copy.start()
            copies.append(copy)
            at += 1
        for copy in copies:
            copy.wait()
        value = slot[0]
        for i in range(1, count):
            value = value + slot[i]
    total_ref[...] = value


def mesh_sum(tile):
    counts = tuple(lax.axis_size(axis) for axis in AXES)
    peers = sum(counts) - len(counts)
    return pl.pallas_call(
        functools.partial(sum_kernel, counts),
        out_shape=jax.ShapeDtypeStruct(tile.shape, tile.dtype),
        in_specs=[pl.BlockSpec(memory_space=pltpu.VMEM)],
        out_specs=pl.BlockSpec(memory_space=pltpu.VMEM),
        scratch_shapes=[pltpu.VMEM((count,) + tile.shape, tile.dtype) for count in counts]
        + [pltpu.SemaphoreType.DMA((peers,)), pltpu.SemaphoreType.DMA((peers,))],
        compiler_params=pltpu.CompilerParams(collective_id=0, has_side_effects=True),
    )(tile)


def per_device(displacement, velocity, body_force, broken):
    rows, width = displacement.shape[1], displacement.shape[3]
    first_force, unused = bond_sum(displacement, broken, False)
    first_acceleration = first_force + body_force
    new_displacement = (
        displacement + TIME_STEP * velocity + 0.5 * TIME_STEP * TIME_STEP * first_acceleration
    )
    second_force, local_energy = bond_sum(new_displacement, broken, True)
    new_acceleration = second_force + body_force
    new_velocity = velocity + 0.5 * TIME_STEP * (first_acceleration + new_acceleration)
    total_energy = jnp.sum(mesh_sum(local_energy))
    area = rows * lax.axis_size("gx") * width * lax.axis_size("gy")
    strain_energy = total_energy / jnp.float32(area)
    return (new_displacement, new_velocity, new_acceleration, strain_energy)


def solution(mesh):
    spec = P(None, "gx", "gz", "gy")
    return jax.shard_map(
        per_device,
        mesh=mesh,
        in_specs=(spec,) * 4,
        out_specs=(spec, spec, spec, P()),
        check_vma=False,
    )
```

profile of v0, /device:TPU:0, one launch (start us, length us, event | category | flops | bytes accessed | tf_op | source)
XLA Modules:
  0.0 89.4 jit_solution(7271818565743848953)
XLA Ops:
  0.6 0.8 fusion.5
  1.5 3.0 %collective-permute-start = (f32[3,3,8,128]{3,2,1,0:T(8,128)S(1)}, f32[3,3,8,128]{3,2,1,0:T(8,128)S(1)}, u32[]{:S(2)}, u32[]{:S(2)}) collective-permute-start(f32[3,3,8,128]{3,2,1,0:T(8,128)S(1)} %get-tuple-element.25), channel_id=1, source_target_pairs={{0,16},{16,0},{1,17},{17,1},{2,18},{18,2},{3,19},{19,3},{4,20},{20... | collective-permute-start | bytes 110600 | tf_op jit(solution)/shard_map/ppermute | solution.py:27
  4.5 1.9 %collective-permute-done = f32[3,3,8,128]{3,2,1,0:T(8,128)S(1)} collective-permute-done((f32[3,3,8,128]{3,2,1,0:T(8,128)S(1)}, f32[3,3,8,128]{3,2,1,0:T(8,128)S(1)}, u32[]{:S(2)}, u32[]{:S(2)}) %collective-permute-start) | collective-permute-done | bytes 36896 | tf_op jit(solution)/shard_map/ppermute | solution.py:27
  6.4 2.0 %collective-permute-done.1 = f32[3,3,8,128]{3,2,1,0:T(8,128)S(1)} collective-permute-done((f32[3,3,8,128]{3,2,1,0:T(8,128)S(1)}, f32[3,3,8,128]{3,2,1,0:T(8,128)S(1)}, u32[]{:S(2)}, u32[]{:S(2)}) %collective-permute-start.1) | collective-permute-done | bytes 36896 | tf_op jit(solution)/shard_map/ppermute | solution.py:30
  8.4 1.6 %collective-permute-start.2 = (f32[3,14,3,128]{3,2,1,0:T(4,128)S(1)}, f32[3,14,3,128]{3,2,1,0:T(4,128)S(1)}, u32[]{:S(2)}, u32[]{:S(2)}) collective-permute-start(f32[3,14,3,128]{3,2,1,0:T(4,128)S(1)} %get-tuple-element.20), channel_id=1, source_target_pairs={{0,1},{1,2},{2,3},{3,0},{4,5},{5,6},{6,7},{7,4},{8,9},{9,10},{10,1... | collective-permute-start | bytes 193544 | tf_op jit(solution)/shard_map/ppermute | solution.py:27
  10.1 2.2 %collective-permute-start.3 = (f32[3,14,3,128]{3,2,1,0:T(4,128)S(1)}, f32[3,14,3,128]{3,2,1,0:T(4,128)S(1)}, u32[]{:S(2)}, u32[]{:S(2)}) collective-permute-start(f32[3,14,3,128]{3,2,1,0:T(4,128)S(1)} %get-tuple-element.21), channel_id=1, source_target_pairs={{1,0},{2,1},{3,2},{0,3},{5,4},{6,5},{7,6},{4,7},{9,8},{10,9},{11,1... | collective-permute-start | bytes 193544 | tf_op jit(solution)/shard_map/ppermute | solution.py:30
  12.3 3.0 %collective-permute-done.2 = f32[3,14,3,128]{3,2,1,0:T(4,128)S(1)} collective-permute-done((f32[3,14,3,128]{3,2,1,0:T(4,128)S(1)}, f32[3,14,3,128]{3,2,1,0:T(4,128)S(1)}, u32[]{:S(2)}, u32[]{:S(2)}) %collective-permute-start.2) | collective-permute-done | bytes 64544 | tf_op jit(solution)/shard_map/ppermute | solution.py:27
  16.4 6.9 %collective-permute-done.4 = f32[3,14,14,3]{3,2,1,0:T(8,128)S(1)} collective-permute-done((f32[3,14,14,3]{3,2,1,0:T(8,128)S(1)}, f32[3,14,14,3]{3,2,1,0:T(8,128)S(1)}, u32[]{:S(2)}, u32[]{:S(2)}) %collective-permute-start.4) | collective-permute-done | bytes 7088 | tf_op jit(solution)/shard_map/ppermute | solution.py:30
  23.2 3.0 %collective-permute-done.5 = f32[3,14,14,3]{3,2,1,0:T(8,128)S(1)} collective-permute-done((f32[3,14,14,3]{3,2,1,0:T(8,128)S(1)}, f32[3,14,14,3]{3,2,1,0:T(8,128)S(1)}, u32[]{:S(2)}, u32[]{:S(2)}) %collective-permute-start.5) | collective-permute-done | bytes 7088 | tf_op jit(solution)/shard_map/ppermute | solution.py:27
  26.4 11.8 %shard_map.75 = (f32[3,8,8,128]{3,2,1,0:T(8,128)S(1)}, f32[8,128]{1,0:T(8,128)}) custom-call(f32[3,14,14,128]{3,2,1,0:T(8,128)S(1)} %pad_maximum_fusion.a_ref, f32[3,14,14,128]{3,2,1,0:T(8,128)S(1)} %pad_maximum_fusion.1.b_ref, s32[12,8,8,128]{3,2,1,0:T(8,128)S(1)} %copy-done), custom_call_target="tpu_custom_call" | custom-call | tf_op jit(solution)/shard_map/pallas_call | solution.py:155
  38.2 0.6 collective-permute-start.6
  38.8 1.5 %collective-permute-start.7 = (f32[3,3,8,128]{3,2,1,0:T(8,128)S(1)}, f32[3,3,8,128]{3,2,1,0:T(8,128)S(1)}, u32[]{:S(2)}, u32[]{:S(2)}) collective-permute-start(f32[3,3,8,128]{3,2,1,0:T(8,128)S(1)} %get-tuple-element.23), channel_id=1, source_target_pairs={{16,0},{0,16},{17,1},{1,17},{18,2},{2,18},{19,3},{3,19},{20,4},{4,... | collective-permute-start | bytes 110600 | tf_op jit(solution)/shard_map/ppermute | solution.py:30
  40.3 1.9 %collective-permute-done.6 = f32[3,3,8,128]{3,2,1,0:T(8,128)S(1)} collective-permute-done((f32[3,3,8,128]{3,2,1,0:T(8,128)S(1)}, f32[3,3,8,128]{3,2,1,0:T(8,128)S(1)}, u32[]{:S(2)}, u32[]{:S(2)}) %collective-permute-start.6) | collective-permute-done | bytes 36896 | tf_op jit(solution)/shard_map/ppermute | solution.py:27
  42.3 0.5 collective-permute-done.7
  42.8 1.1 %collective-permute-start.8 = (f32[3,14,3,128]{3,2,1,0:T(4,128)S(1)}, f32[3,14,3,128]{3,2,1,0:T(4,128)S(1)}, u32[]{:S(2)}, u32[]{:S(2)}) collective-permute-start(f32[3,14,3,128]{3,2,1,0:T(4,128)S(1)} %get-tuple-element.18), channel_id=1, source_target_pairs={{0,1},{1,2},{2,3},{3,0},{4,5},{5,6},{6,7},{7,4},{8,9},{9,10},{10,1... | collective-permute-start | bytes 193544 | tf_op jit(solution)/shard_map/ppermute | solution.py:27
  43.9 2.8 %collective-permute-start.9 = (f32[3,14,3,128]{3,2,1,0:T(4,128)S(1)}, f32[3,14,3,128]{3,2,1,0:T(4,128)S(1)}, u32[]{:S(2)}, u32[]{:S(2)}) collective-permute-start(f32[3,14,3,128]{3,2,1,0:T(4,128)S(1)} %get-tuple-element.19), channel_id=1, source_target_pairs={{1,0},{2,1},{3,2},{0,3},{5,4},{6,5},{7,6},{4,7},{9,8},{10,9},{11,1... | collective-permute-start | bytes 193544 | tf_op jit(solution)/shard_map/ppermute | solution.py:30
  46.7 2.6 %collective-permute-done.8 = f32[3,14,3,128]{3,2,1,0:T(4,128)S(1)} collective-permute-done((f32[3,14,3,128]{3,2,1,0:T(4,128)S(1)}, f32[3,14,3,128]{3,2,1,0:T(4,128)S(1)}, u32[]{:S(2)}, u32[]{:S(2)}) %collective-permute-start.8) | collective-permute-done | bytes 64544 | tf_op jit(solution)/shard_map/ppermute | solution.py:27
  50.1 7.9 %collective-permute-done.10 = f32[3,14,14,3]{3,2,1,0:T(8,128)S(1)} collective-permute-done((f32[3,14,14,3]{3,2,1,0:T(8,128)S(1)}, f32[3,14,14,3]{3,2,1,0:T(8,128)S(1)}, u32[]{:S(2)}, u32[]{:S(2)}) %collective-permute-start.10) | collective-permute-done | bytes 7088 | tf_op jit(solution)/shard_map/ppermute | solution.py:30
  58.1 1.0 %collective-permute-done.11 = f32[3,14,14,3]{3,2,1,0:T(8,128)S(1)} collective-permute-done((f32[3,14,14,3]{3,2,1,0:T(8,128)S(1)}, f32[3,14,14,3]{3,2,1,0:T(8,128)S(1)}, u32[]{:S(2)}, u32[]{:S(2)}) %collective-permute-start.11) | collective-permute-done | bytes 7088 | tf_op jit(solution)/shard_map/ppermute | solution.py:27
  59.2 12.4 %shard_map.76 = (f32[3,8,8,128]{3,2,1,0:T(8,128)S(1)}, f32[8,128]{1,0:T(8,128)S(1)}) custom-call(f32[3,14,14,128]{3,2,1,0:T(8,128)S(1)} %pad_maximum_fusion.2.a_ref, f32[3,14,14,128]{3,2,1,0:T(8,128)S(1)} %pad_maximum_fusion.3.b_ref, s32[12,8,8,128]{3,2,1,0:T(8,128)S(1)} %copy-done), custom_call_target="tpu_custom_call" | custom-call | tf_op jit(solution)/shard_map/pallas_call | solution.py:155
  71.6 0.6 copy-done.1
  72.2 13.4 %shard_map.77 = f32[8,128]{1,0:T(8,128)} custom-call(f32[8,128]{1,0:T(8,128)} %copy-done.1), custom_call_target="tpu_custom_call" | custom-call | tf_op jit(solution)/shard_map/pallas_call | solution.py:219
  85.7 1.3 %reduce_sum.9 = f32[]{:T(128)} reduce(f32[8,128]{1,0:T(8,128)} %shard_map.77, f32[]{:T(128)} %constant.1.clone.1), dimensions={0,1}, to_apply=%region_0.0 | reduce | flops 1023 | bytes 4104 | tf_op jit(solution)/shard_map/reduce_sum | solution.py:240
  87.0 0.7 multiply_add_fusion
  (34 shorter events, 2.4 us)
Async XLA Ops:
  0.6 5.8 %copy-start.3 = (f32[3,8,8,128]{3,2,1,0:T(8,128)S(1)}, f32[3,8,8,128]{3,2,1,0:T(8,128)}, u32[]{:S(2)}) copy-start(f32[3,8,8,128]{3,2,1,0:T(8,128)} %param.4) | copy-start | bytes 294916
  1.5 4.9 %collective-permute-start = (f32[3,3,8,128]{3,2,1,0:T(8,128)S(1)}, f32[3,3,8,128]{3,2,1,0:T(8,128)S(1)}, u32[]{:S(2)}, u32[]{:S(2)}) collective-permute-start(f32[3,3,8,128]{3,2,1,0:T(8,128)S(1)} %get-tuple-element.25), channel_id=1, source_target_pairs={{0,16},{16,0},{1,17},{17,1},{2,18},{18,2},{3,19},{19,3},{4,20},{20... | collective-permute-start | bytes 110600 | tf_op jit(solution)/shard_map/ppermute | solution.py:27
  4.4 4.0 %collective-permute-start.1 = (f32[3,3,8,128]{3,2,1,0:T(8,128)S(1)}, f32[3,3,8,128]{3,2,1,0:T(8,128)S(1)}, u32[]{:S(2)}, u32[]{:S(2)}) collective-permute-start(f32[3,3,8,128]{3,2,1,0:T(8,128)S(1)} %get-tuple-element.24), channel_id=1, source_target_pairs={{16,0},{0,16},{17,1},{1,17},{18,2},{2,18},{19,3},{3,19},{20,4},{4,... | collective-permute-start | bytes 110600 | tf_op jit(solution)/shard_map/ppermute | solution.py:30
  8.4 6.9 %collective-permute-start.2 = (f32[3,14,3,128]{3,2,1,0:T(4,128)S(1)}, f32[3,14,3,128]{3,2,1,0:T(4,128)S(1)}, u32[]{:S(2)}, u32[]{:S(2)}) collective-permute-start(f32[3,14,3,128]{3,2,1,0:T(4,128)S(1)} %get-tuple-element.20), channel_id=1, source_target_pairs={{0,1},{1,2},{2,3},{3,0},{4,5},{5,6},{6,7},{7,4},{8,9},{9,10},{10,1... | collective-permute-start | bytes 193544 | tf_op jit(solution)/shard_map/ppermute | solution.py:27
  10.1 5.4 %collective-permute-start.3 = (f32[3,14,3,128]{3,2,1,0:T(4,128)S(1)}, f32[3,14,3,128]{3,2,1,0:T(4,128)S(1)}, u32[]{:S(2)}, u32[]{:S(2)}) collective-permute-start(f32[3,14,3,128]{3,2,1,0:T(4,128)S(1)} %get-tuple-element.21), channel_id=1, source_target_pairs={{1,0},{2,1},{3,2},{0,3},{5,4},{6,5},{7,6},{4,7},{9,8},{10,9},{11,1... | collective-permute-start | bytes 193544 | tf_op jit(solution)/shard_map/ppermute | solution.py:30
  15.7 7.5 %collective-permute-start.4 = (f32[3,14,14,3]{3,2,1,0:T(8,128)S(1)}, f32[3,14,14,3]{3,2,1,0:T(8,128)S(1)}, u32[]{:S(2)}, u32[]{:S(2)}) collective-permute-start(f32[3,14,14,3]{3,2,1,0:T(8,128)S(1)} %get-tuple-element.16), channel_id=1, source_target_pairs={{4,0},{8,4},{12,8},{0,12},{5,1},{9,5},{13,9},{1,13},{6,2},{10,6},{... | collective-permute-start | bytes 21176 | tf_op jit(solution)/shard_map/ppermute | solution.py:30
  15.8 10.4 %collective-permute-start.5 = (f32[3,14,14,3]{3,2,1,0:T(8,128)S(1)}, f32[3,14,14,3]{3,2,1,0:T(8,128)S(1)}, u32[]{:S(2)}, u32[]{:S(2)}) collective-permute-start(f32[3,14,14,3]{3,2,1,0:T(8,128)S(1)} %get-tuple-element.17), channel_id=1, source_target_pairs={{0,4},{4,8},{8,12},{12,0},{1,5},{5,9},{9,13},{13,1},{2,6},{6,10},{... | collective-permute-start | bytes 21176 | tf_op jit(solution)/shard_map/ppermute | solution.py:27
  16.4 10.0 %copy-start = (s32[12,8,8,128]{3,2,1,0:T(8,128)S(1)}, s32[12,8,8,128]{3,2,1,0:T(8,128)}, u32[]{:S(2)}) copy-start(s32[12,8,8,128]{3,2,1,0:T(8,128)} %broken_ref.3) | copy-start | bytes 1179652
  26.4 11.8 %copy-start.4 = (f32[3,8,8,128]{3,2,1,0:T(8,128)S(1)}, f32[3,8,8,128]{3,2,1,0:T(8,128)}, u32[]{:S(2)}) copy-start(f32[3,8,8,128]{3,2,1,0:T(8,128)} %param.5) | copy-start | bytes 294916
  26.4 11.8 %copy-start.5 = (f32[3,8,8,128]{3,2,1,0:T(8,128)S(1)}, f32[3,8,8,128]{3,2,1,0:T(8,128)}, u32[]{:S(2)}) copy-start(f32[3,8,8,128]{3,2,1,0:T(8,128)} %param.6) | copy-start | bytes 294916
  38.2 11.1 %copy-start.2 = (f32[3,8,8,128]{3,2,1,0:T(8,128)}, f32[3,8,8,128]{3,2,1,0:T(8,128)S(1)}, u32[]{:S(2)}) copy-start(f32[3,8,8,128]{3,2,1,0:T(8,128)S(1)} %get-tuple-element.12) | copy-start | bytes 294916
  38.2 4.0 %collective-permute-start.6 = (f32[3,3,8,128]{3,2,1,0:T(8,128)S(1)}, f32[3,3,8,128]{3,2,1,0:T(8,128)S(1)}, u32[]{:S(2)}, u32[]{:S(2)}) collective-permute-start(f32[3,3,8,128]{3,2,1,0:T(8,128)S(1)} %get-tuple-element.22), channel_id=1, source_target_pairs={{0,16},{16,0},{1,17},{17,1},{2,18},{18,2},{3,19},{19,3},{4,20},{20... | collective-permute-start | bytes 110600 | tf_op jit(solution)/shard_map/ppermute | solution.py:27
  38.8 4.0 %collective-permute-start.7 = (f32[3,3,8,128]{3,2,1,0:T(8,128)S(1)}, f32[3,3,8,128]{3,2,1,0:T(8,128)S(1)}, u32[]{:S(2)}, u32[]{:S(2)}) collective-permute-start(f32[3,3,8,128]{3,2,1,0:T(8,128)S(1)} %get-tuple-element.23), channel_id=1, source_target_pairs={{16,0},{0,16},{17,1},{1,17},{18,2},{2,18},{19,3},{3,19},{20,4},{4,... | collective-permute-start | bytes 110600 | tf_op jit(solution)/shard_map/ppermute | solution.py:30
  42.8 6.4 %collective-permute-start.8 = (f32[3,14,3,128]{3,2,1,0:T(4,128)S(1)}, f32[3,14,3,128]{3,2,1,0:T(4,128)S(1)}, u32[]{:S(2)}, u32[]{:S(2)}) collective-permute-start(f32[3,14,3,128]{3,2,1,0:T(4,128)S(1)} %get-tuple-element.18), channel_id=1, source_target_pairs={{0,1},{1,2},{2,3},{3,0},{4,5},{5,6},{6,7},{7,4},{8,9},{9,10},{10,1... | collective-permute-start | bytes 193544 | tf_op jit(solution)/shard_map/ppermute | solution.py:27
  43.9 5.4 %collective-permute-start.9 = (f32[3,14,3,128]{3,2,1,0:T(4,128)S(1)}, f32[3,14,3,128]{3,2,1,0:T(4,128)S(1)}, u32[]{:S(2)}, u32[]{:S(2)}) collective-permute-start(f32[3,14,3,128]{3,2,1,0:T(4,128)S(1)} %get-tuple-element.19), channel_id=1, source_target_pairs={{1,0},{2,1},{3,2},{0,3},{5,4},{6,5},{7,6},{4,7},{9,8},{10,9},{11,1... | collective-permute-start | bytes 193544 | tf_op jit(solution)/shard_map/ppermute | solution.py:30
  49.6 8.5 %collective-permute-start.10 = (f32[3,14,14,3]{3,2,1,0:T(8,128)S(1)}, f32[3,14,14,3]{3,2,1,0:T(8,128)S(1)}, u32[]{:S(2)}, u32[]{:S(2)}) collective-permute-start(f32[3,14,14,3]{3,2,1,0:T(8,128)S(1)} %get-tuple-element.14), channel_id=1, source_target_pairs={{4,0},{8,4},{12,8},{0,12},{5,1},{9,5},{13,9},{1,13},{6,2},{10,6},{... | collective-permute-start | bytes 21176 | tf_op jit(solution)/shard_map/ppermute | solution.py:30
  49.7 9.4 %collective-permute-start.11 = (f32[3,14,14,3]{3,2,1,0:T(8,128)S(1)}, f32[3,14,14,3]{3,2,1,0:T(8,128)S(1)}, u32[]{:S(2)}, u32[]{:S(2)}) collective-permute-start(f32[3,14,14,3]{3,2,1,0:T(8,128)S(1)} %get-tuple-element.15), channel_id=1, source_target_pairs={{0,4},{4,8},{8,12},{12,0},{1,5},{5,9},{9,13},{13,1},{2,6},{6,10},{... | collective-permute-start | bytes 21176 | tf_op jit(solution)/shard_map/ppermute | solution.py:27
  71.6 0.6 copy-start.1
where the time goes:
time: 89.7 us; the launch traced here: 89.4 us
  Pallas kernels  37.6 us (42%)
  waiting for transfers between devices  30.9 us (34%)
  starting transfers between devices  14 us (16%)
  between operations  2.57 us (3%)
  other arithmetic  2.47 us (3%)
  local copies, waits for them, and re-layouts  1.94 us (2%)
    pallas_call x2, Pallas kernels, bond_sum(): pl.pallas_call(functools.partial(pass_kernel, depth_total, with_energy),...  24.2 us
    ppermute x6, waiting for transfers between devices, extended(): high = lax.ppermute(lax.slice_in_dim(block, 0, W, axis=dim), axis, backward)  17.6 us
    pallas_call x1, Pallas kernels, mesh_sum(): pl.pallas_call(functools.partial(sum_kernel, counts), out_shape=jax.Shape...  13.4 us
    ppermute x6, waiting for transfers between devices, extended(): lax.ppermute(lax.slice_in_dim(block, block.shape[dim] - W, None, axis=dim...  13.3 us
    ppermute x6, starting transfers between devices, extended(): lax.ppermute(lax.slice_in_dim(block, block.shape[dim] - W, None, axis=dim...  7.28 us
    ppermute x6, starting transfers between devices, extended(): high = lax.ppermute(lax.slice_in_dim(block, 0, W, axis=dim), axis, backward)  6.71 us
  transfers between devices with their start and end apart: 12, of which 12 were waited for; matrix products, arithmetic and copies ran while one was open for 0% of the time, Pallas kernels for 0%

commit v1 on v0

v1 whole, which is shorter than its diff:
```python
import functools
import math

import jax
import jax.numpy as jnp
from jax import lax
from jax.experimental import pallas as pl
from jax.experimental.pallas import tpu as pltpu
from jax.sharding import PartitionSpec as P

TIME_STEP = 0.05
MICRO_MODULUS = 4.0
BITS_PER_WORD = 30
W = 3
REACH = range(-W, W + 1)
BONDS = tuple(
    (p, q, r) for p in REACH for q in REACH for r in REACH if (p, q, r) != (0, 0, 0)
)
INDEX = {bond: k for k, bond in enumerate(BONDS)}
WORD_COUNT = -(-len(BONDS) // BITS_PER_WORD)
AXES = ("gx", "gy", "gz")
MESH = pl.DeviceIdType.MESH
HIGH, LOW = 0, 1
SIDES = (-1, 1)


def align(n):
    return -(-n // 8) * 8


def depth_bits(shape, depth_start, depth_total):
    depth = lax.broadcasted_iota(jnp.int32, shape, 0) + depth_start
    words = [jnp.zeros(shape, jnp.int32) for _ in range(WORD_COUNT)]
    for q in REACH:
        if q == 0:
            continue
        outside = (depth + q < 0) | (depth + q >= depth_total)
        for w in range(WORD_COUNT):
            bits = 0
            for (p, q2, r), k in INDEX.items():
                if q2 == q and k // BITS_PER_WORD == w:
                    bits |= 1 << (k % BITS_PER_WORD)
            if bits:
                words[w] = words[w] | jnp.where(outside, bits, 0)
    return words


def store_masks(broken_ref, mask_ref, outside_ref, depth_start, depth_total):
    rows = broken_ref.shape[1]
    for w, word in enumerate(depth_bits(broken_ref.shape[2:], depth_start, depth_total)):
        outside_ref[w] = word

    def body(x, carry):
        for w in range(WORD_COUNT):
            word = broken_ref[w, x] | outside_ref[w]
            for k in range(w * BITS_PER_WORD, min(len(BONDS), (w + 1) * BITS_PER_WORD)):
                p, q, r = BONDS[k]
                weight = MICRO_MODULUS * math.exp(-(p * p + q * q + r * r) / 9.0)
                bit = word & (1 << (k % BITS_PER_WORD))
                mask_ref[k, x] = jnp.where(bit == 0, jnp.float32(weight), jnp.float32(0.0))
        return carry

    lax.fori_loop(0, rows, body, 0)


def row_bonds(p, x, e_ref, mask_ref, acc_ref, depth, energy):
    center = [e_ref[W, c, x + W, W : W + depth] for c in range(3)]
    force = [acc_ref[c, x] for c in range(3)]
    center_x = center[0] - float(p)
    center_z = {q: center[1] - float(q) for q in REACH}
    classes = {}
    for q in REACH:
        for r in REACH:
            if (p, q, r) != (0, 0, 0):
                key = 0 if energy is None else q * q + r * r
                classes.setdefault(key, []).append((q, r))
    for key in sorted(classes):
        part = None
        for q, r in classes[key]:
            rest = math.sqrt(p * p + q * q + r * r)
            nb = [e_ref[r + W, c, x + (W + p), W + q : W + q + depth] for c in range(3)]
            bx = nb[0] - center_x
            bz = nb[1] - center_z[q]
            by = nb[2] - center[2]
            square = bx * bx + bz * bz + by * by
            h = jnp.float32(1.0 / rest) - lax.rsqrt(square)
            g = mask_ref[INDEX[p, q, r], x] * h
            force[0] = force[0] + g * bx
            force[1] = force[1] + g * bz
            force[2] = force[2] + g * by
            if energy is not None:
                e = g * (h * square)
                part = e if part is None else part + e
        if energy is not None:
            energy = energy + part * jnp.float32(0.25 * rest)
    for c in range(3):
        acc_ref[c, x] = force[c]
    return energy


def step_kernel(
    counts, depth_total, area,
    disp_hbm, vel_hbm, body_hbm, broken_hbm,
    new_disp_ref, new_vel_ref, new_acc_ref, energy_ref,
    disp_ref, vel_ref, body_ref, broken_ref, acc_ref,
    e1_ref, e2_ref, mask_ref, outside_ref,
    slab_ref, pack_ref, own_z, own_0, far_z, far_0, far_x,
    slot_x, slot_y, slot_z, etile_ref,
    in_sem, recv_sem, send_sem, esend_sem, erecv_sem,
):
    nx, ny, nz = counts
    _, rows, depth, width = disp_ref.shape
    ix, iy, iz = (lax.axis_index(axis) for axis in AXES)
    has_z = {-1: iz > 0, 1: iz < nz - 1}
    group_rows = {
        HIGH: list(range(rows - W, rows)) + list(range(W, rows - W)),
        LOW: list(range(W)),
    }
    slab_rows = {g: align(9 * len(group_rows[g])) for g in (HIGH, LOW)}
    far_rows = align(9 * W)
    toward = {HIGH: 1, LOW: -1}

    def device(dx, dy, dz):
        where = {}
        if dx:
            where["gx"] = lax.rem(ix + (dx + nx), nx)
        if dy:
            where["gy"] = lax.rem(iy + (dy + ny), ny)
        if dz:
            where["gz"] = iz + dz
        return where

    inputs = [
        pltpu.make_async_copy(src, dst, in_sem.at[i])
        for i, (src, dst) in enumerate(
            ((disp_hbm, disp_ref), (broken_hbm, broken_ref), (vel_hbm, vel_ref), (body_hbm, body_ref))
        )
    ]
    for copy in inputs:
        copy.start()

    for s, dz in enumerate(SIDES):

        @pl.when(jnp.logical_not(has_z[dz]))
        def _(s=s):
            for ex in range(2):
                for g in (HIGH, LOW):
                    own_z[ex, g, s] = jnp.zeros(own_z.shape[3:], jnp.float32)
                    far_z[ex, g, s] = jnp.zeros(far_z.shape[3:], jnp.float32)

    barrier = pltpu.get_barrier_semaphore()
    dxs = (0, 1) if nx == 2 else (-1, 0, 1)
    sure = 0
    maybe = {-1: 0, 1: 0}
    for dz in (-1, 0, 1):
        for dx in dxs:
            for dy in (-1, 0, 1):
                if (dx, dy, dz) == (0, 0, 0):
                    continue

                def greet(dx=dx, dy=dy, dz=dz):
                    pl.semaphore_signal(
                        barrier, inc=1, device_id=device(dx, dy, dz), device_id_type=MESH
                    )

                if dz == 0:
                    greet()
                    sure += 1
                else:
                    pl.when(has_z[dz])(greet)
                    maybe[dz] += 1
    for axis, count, me in zip(AXES, counts, (ix, iy, iz)):
        for d in range(1, count):
            pl.semaphore_signal(
                barrier, inc=1, device_id={axis: lax.rem(me + d, count)}, device_id_type=MESH
            )
            sure += 1

    lane = lax.broadcasted_iota(jnp.int32, (depth, width), 1)

    def stage(ex, g, src):
        pack = jnp.zeros((depth, width), jnp.float32)
        for k, x in enumerate(group_rows[g]):
            for c in range(3):
                tile = src[c, x]
                at = 9 * k + 3 * c
                slab_ref[ex, g, 0, at : at + W] = tile[:W]
                slab_ref[ex, g, 1, at : at + W] = tile[depth - W :]
                at = 6 * (3 * k + c)
                moved = pltpu.roll(tile, W + at, 1)
                pack = jnp.where((lane >= at) & (lane < at + 2 * W), moved, pack)
        pack_ref[ex, g] = pack

    def copies(ex, g, src):
        out = []

        def add(src_ref, dst_ref, kind, dx, dy, dz):
            out.append(
                (
                    dz,
                    pltpu.make_async_remote_copy(
                        src_ref=src_ref,
                        dst_ref=dst_ref,
                        send_sem=send_sem.at[ex, g, len(out)],
                        recv_sem=recv_sem.at[ex, g, kind],
                        device_id=device(dx, dy, dz),
                        device_id_type=MESH,
                    ),
                )
            )

        n = slab_rows[g]
        t = toward[g]
        for s, dz in enumerate(SIDES):
            add(slab_ref.at[ex, g, s, 0:n], own_z.at[ex, g, 1 - s, 0:n], 1 - s, 0, 0, dz)
        for i, dy in enumerate(SIDES):
            edge = pl.ds(8 * (1 - i), 8)
            add(pack_ref.at[ex, g], own_0.at[ex, g, edge], 2, 0, dy, 0)
            for s, dz in enumerate(SIDES):
                edge = pl.ds(n + 8 * (1 - i), 8)
                add(pack_ref.at[ex, g], own_z.at[ex, g, 1 - s, edge], 1 - s, 0, dy, dz)
        first = rows - W if g == HIGH else 0
        add(src.at[:, first : first + W], far_x.at[ex, g], 6, t, 0, 0)
        for s, dz in enumerate(SIDES):
            add(
                slab_ref.at[ex, g, s, 0:far_rows], far_z.at[ex, g, 1 - s, 0:far_rows],
                3 + 1 - s, t, 0, dz,
            )
        for i, dy in enumerate(SIDES):
            edge = pl.ds(8 * (1 - i), 8)
            add(pack_ref.at[ex, g], far_0.at[ex, g, edge], 5, t, dy, 0)
            for s, dz in enumerate(SIDES):
                edge = pl.ds(far_rows + 8 * (1 - i), 8)
                add(pack_ref.at[ex, g], far_z.at[ex, g, 1 - s, edge], 3 + 1 - s, t, dy, dz)
        return out

    def each(pairs, act):
        for want in (0, -1, 1):

            def run(want=want):
                for dz, copy in pairs:
                    if dz == want:
                        act(copy)

            if want == 0:
                run()
            else:
                pl.when(has_z[want])(run)

    def arrived(ref, ex, g, kind):
        pltpu.make_async_copy(ref, ref, recv_sem.at[ex, g, kind]).wait()

    def wait_own(ex, g):
        arrived(own_0.at[ex, g], ex, g, 2)
        for s, dz in enumerate(SIDES):
            pl.when(has_z[dz])(
                functools.partial(
                    arrived, own_z.at[ex, g, s, 0 : slab_rows[g] + 16], ex, g, s
                )
            )

    def wait_far(ex, g):
        arrived(far_0.at[ex, g], ex, g, 5)
        arrived(far_x.at[ex, g], ex, g, 6)
        for s, dz in enumerate(SIDES):
            pl.when(has_z[dz])(
                functools.partial(arrived, far_z.at[ex, g, s, 0 : far_rows + 16], ex, g, 3 + s)
            )

    padded = e1_ref.shape[3]
    wide = lax.broadcasted_iota(jnp.int32, (padded, width), 1)

    def fill(e_ref, ex, g, k, row, far, src):
        z_ref, zero_ref = (far_z, far_0) if far else (own_z, own_0)
        n = far_rows if far else slab_rows[g]
        edges = []
        for i in range(2):
            below = z_ref[ex, g, 0, n + 8 * i : n + 8 * i + 8]
            here = zero_ref[ex, g, 8 * i : 8 * i + 8]
            above = z_ref[ex, g, 1, n + 8 * i : n + 8 * i + 8]
            spare = jnp.zeros((padded - depth - 2 * W, width), jnp.float32)
            edges.append(
                jnp.concatenate([below[depth - W :], here, above[:W], spare], axis=0)
            )
        for c in range(3):
            at = 9 * k + 3 * c
            tile = jnp.concatenate(
                [
                    z_ref[ex, g, 0, at : at + W],
                    src(c),
                    z_ref[ex, g, 1, at : at + W],
                    jnp.zeros((padded - depth - 2 * W, width), jnp.float32),
                ],
                axis=0,
            )
            at = 6 * (3 * k + c)
            side = jnp.where(
                wide < W,
                pltpu.roll(edges[1], (2 * width - at - W) % width, 1),
                pltpu.roll(edges[0], (2 * width - W - at) % width, 1),
            )
            for r in REACH:
                if r == 0:
                    moved = tile
                elif r > 0:
                    moved = pltpu.roll(jnp.where(wide < r, side, tile), width - r, 1)
                else:
                    moved = pltpu.roll(jnp.where(wide >= width + r, side, tile), -r, 1)
                if c == 2 and r != 0:
                    moved = moved + float(r)
                e_ref[r + W, c, row] = moved

    def fill_own(e_ref, ex, g, src):
        for k, x in enumerate(group_rows[g]):
            fill(e_ref, ex, g, k, x + W, False, lambda c, x=x: src[c, x])

    def fill_far(e_ref, ex, g):
        for k in range(W):
            row = k if g == HIGH else rows + W + k
            fill(e_ref, ex, g, k, row, True, lambda c, k=k: far_x[ex, g, c, k])

    inputs[0].wait()
    for g in (HIGH, LOW):
        stage(0, g, disp_ref)

    expected = sure
    for dz in SIDES:
        expected = expected + jnp.where(has_z[dz], maybe[dz], 0)
    pl.semaphore_wait(barrier, expected)

    for g in (HIGH, LOW):
        each(copies(0, g, disp_ref), lambda copy: copy.start())

    inputs[1].wait()
    store_masks(broken_ref, mask_ref, outside_ref, iz * depth, depth_total)
    inputs[2].wait()
    inputs[3].wait()
    acc_ref[...] = body_ref[...]
    new_acc_ref[...] = body_ref[...]
    etile_ref[...] = jnp.zeros_like(etile_ref)

    for g in (HIGH, LOW):
        wait_own(0, g)
    for g in (HIGH, LOW):
        fill_own(e1_ref, 0, g, disp_ref)

    def first(i, carry):
        @pl.when(i == rows - 2 * W)
        def _():
            for g in (HIGH, LOW):
                wait_far(0, g)
            for g in (HIGH, LOW):
                fill_far(e1_ref, 0, g)

        x = lax.rem(i + W, rows)
        for p in REACH:
            row_bonds(p, x, e1_ref, mask_ref, acc_ref, depth, None)
        for c in range(3):
            a = acc_ref[c, x]
            v = vel_ref[c, x]
            new_disp_ref[c, x] = (
                disp_ref[c, x] + TIME_STEP * v + 0.5 * TIME_STEP * TIME_STEP * a
            )
            new_vel_ref[c, x] = v + 0.5 * TIME_STEP * a

        @pl.when(i == rows - W - 1)
        def _():
            stage(1, HIGH, new_disp_ref)
            each(copies(1, HIGH, new_disp_ref), lambda copy: copy.start())

        return carry

    lax.fori_loop(0, rows, first, 0)
    stage(1, LOW, new_disp_ref)
    each(copies(1, LOW, new_disp_ref), lambda copy: copy.start())

    def second(j, carry):
        @pl.when(j == 0)
        def _():
            wait_own(1, HIGH)
            fill_own(e2_ref, 1, HIGH, new_disp_ref)
            for c in range(3):
                for x in range(W):
                    e2_ref[W, c, x + W, W : W + depth] = new_disp_ref[c, x]

        @pl.when(j == rows - 2 * W)
        def _():
            wait_far(1, HIGH)
            fill_far(e2_ref, 1, HIGH)

        @pl.when(j == rows - W)
        def _():
            wait_own(1, LOW)
            fill_own(e2_ref, 1, LOW, new_disp_ref)
            wait_far(1, LOW)
            fill_far(e2_ref, 1, LOW)

        energy = jnp.zeros(etile_ref.shape, jnp.float32)
        for p in REACH:
            x = lax.rem(j + (W - p + rows), rows)
            energy = row_bonds(p, x, e2_ref, mask_ref, new_acc_ref, depth, energy)
        etile_ref[...] += energy
        return carry

    lax.fori_loop(0, rows, second, 0)
    for c in range(3):
        for x in range(rows):
            new_vel_ref[c, x] = new_vel_ref[c, x] + 0.5 * TIME_STEP * new_acc_ref[c, x]

    at = 0
    value = etile_ref[...]
    for slot, axis, count, me in zip((slot_x, slot_y, slot_z), AXES, counts, (ix, iy, iz)):
        slot[me] = value
        moves = []
        for d in range(1, count):
            copy = pltpu.make_async_remote_copy(
                src_ref=slot.at[me],
                dst_ref=slot.at[me],
                send_sem=esend_sem.at[at],
                recv_sem=erecv_sem.at[at],
                device_id={axis: lax.rem(me + d, count)},
                device_id_type=MESH,
            )
            copy.start()
            moves.append(copy)
            at += 1
        for copy in moves:
            copy.wait()
        value = slot[0]
        for i in range(1, count):
            value = value + slot[i]
    energy_ref[0, 0] = jnp.sum(value) * jnp.float32(1.0 / area)

    for ex, src in ((0, disp_ref), (1, new_disp_ref)):
        for g in (HIGH, LOW):
            each(copies(ex, g, src), lambda copy: copy.wait_send())


def per_device(displacement, velocity, body_force, broken):
    counts = tuple(lax.axis_size(axis) for axis in AXES)
    _, rows, depth, width = displacement.shape
    area = rows * counts[0] * width * counts[1]
    padded = align(depth + 2 * W)
    slab = align(9 * (rows - W))
    far = align(9 * W)
    peers = sum(counts) - len(counts)
    block = pltpu.VMEM((3, rows, depth, width), jnp.float32)
    out = jax.ShapeDtypeStruct((3, rows, depth, width), jnp.float32)
    vmem = pl.BlockSpec(memory_space=pltpu.VMEM)
    e_shape = pltpu.VMEM((2 * W + 1, 3, rows + 2 * W, padded, width), jnp.float32)
    new_disp, new_vel, new_acc, energy = pl.pallas_call(
        functools.partial(step_kernel, counts, depth * counts[2], area),
        out_shape=(out, out, out, jax.ShapeDtypeStruct((1, 1), jnp.float32)),
        in_specs=[pl.BlockSpec(memory_space=pl.ANY)] * 4,
        out_specs=(vmem, vmem, vmem, pl.BlockSpec(memory_space=pltpu.SMEM)),
        scratch_shapes=[
            block, block, block,
            pltpu.VMEM((broken.shape[0], rows, depth, width), jnp.int32),
            block,
            e_shape, e_shape,
            pltpu.VMEM((len(BONDS), rows, depth, width), jnp.float32),
            pltpu.VMEM((WORD_COUNT, depth, width), jnp.int32),
            pltpu.VMEM((2, 2, 2, slab, width), jnp.float32),
            pltpu.VMEM((2, 2, depth, width), jnp.float32),
            pltpu.VMEM((2, 2, 2, slab + 16, width), jnp.float32),
            pltpu.VMEM((2, 2, 16, width), jnp.float32),
            pltpu.VMEM((2, 2, 2, far + 16, width), jnp.float32),
            pltpu.VMEM((2, 2, 16, width), jnp.float32),
            pltpu.VMEM((2, 2, 3, W, depth, width), jnp.float32),
        ]
        + [pltpu.VMEM((count, depth, width), jnp.float32) for count in counts]
        + [
            pltpu.VMEM((depth, width), jnp.float32),
            pltpu.SemaphoreType.DMA((4,)),
            pltpu.SemaphoreType.DMA((2, 2, 7)),
            pltpu.SemaphoreType.DMA((2, 2, 17)),
            pltpu.SemaphoreType.DMA((peers,)),
            pltpu.SemaphoreType.DMA((peers,)),
        ],
        compiler_params=pltpu.CompilerParams(
            collective_id=0, has_side_effects=True, vmem_limit_bytes=48 * 1024 * 1024
        ),
    )(displacement, velocity, body_force, broken)
    return new_disp, new_vel, new_acc, energy.reshape(())


def solution(mesh):
    spec = P(None, "gx", "gz", "gy")
    return jax.shard_map(
        per_device,
        mesh=mesh,
        in_specs=(spec,) * 4,
        out_specs=(spec, spec, spec, P()),
        check_vma=False,
    )
```

time: 89.7 us -> 48.4 us (0.54)
  waiting for transfers between devices: 30.9 us -> 0 us
  starting transfers between devices: 14 us -> 0 us
  local copies, waits for them, and re-layouts: 1.94 us -> 5.59 us
  Pallas kernels: 37.6 us -> 40.1 us
  other arithmetic: 2.47 us -> 0 us
    ppermute x12 -> x0, waiting for transfers between devices: 30.9 us -> none  [the longest x6 17.6 us: extended(): high = lax.ppermute(lax.slice_in_dim(block, 0, W, axis=dim), axis, backward)]
    ppermute x12 -> x0, starting transfers between devices: 14 us -> none  [the longest x6 7.28 us: extended(): lax.ppermute(lax.slice_in_dim(block, block.shape[dim] - W, None, axis=dim...]
    unnamed x14 -> x11, local copies, waits for them, and re-layouts: 0.63 us -> 5.59 us
    pallas_call x3 -> x1, Pallas kernels: 37.6 us -> 40.1 us  [per_device(): pl.pallas_call(functools.partial(step_kernel, counts, depth * counts[2],...]
    reduce_sum x1 -> x0, other arithmetic: 1.29 us -> none  [per_device(): total_energy = jnp.sum(mesh_sum(local_energy))]
    slice x6 -> x0, local copies, waits for them, and re-layouts: 1.24 us -> none  [the longest x3 1.17 us: extended(): high = lax.ppermute(lax.slice_in_dim(block, 0, W, axis=dim), axis, backward)]
  transfers between devices with their start and end apart: 12 -> 0, of which waited for: 12 -> 0; matrix products, arithmetic and copies ran while one was open for 0% -> 0% of each run, Pallas kernels for 0% -> 0%
where the time goes in v1:
time: 48.4 us; the launch traced here: 48.1 us
  Pallas kernels  40.1 us (83%)
  local copies, waits for them, and re-layouts  5.59 us (12%)
  between operations  2.4 us (5%)
    pallas_call x1, Pallas kernels, per_device(): pl.pallas_call(functools.partial(step_kernel, counts, depth * counts[2],...  40.1 us
    unnamed x11, local copies, waits for them, and re-layouts  5.59 us

profile of v1, /device:TPU:0, one launch (start us, length us, event | category | flops | bytes accessed | tf_op | source)
XLA Modules:
  0.0 48.1 jit_solution(11786680366803186294)
XLA Ops:
  0.6 0.0 copy-start
  0.6 1.0 %copy-done = s32[12,8,8,128]{3,2,1,0:T(8,128)S(1)} copy-done((s32[12,8,8,128]{3,2,1,0:T(8,128)S(1)}, s32[12,8,8,128]{3,2,1,0:T(8,128)}, u32[]{:S(2)}) %copy-start) | copy-done | bytes 393240
  1.6 0.0 copy-start.1
  1.6 0.9 %copy-done.1 = f32[3,8,8,128]{3,2,1,0:T(8,128)S(1)} copy-done((f32[3,8,8,128]{3,2,1,0:T(8,128)S(1)}, f32[3,8,8,128]{3,2,1,0:T(8,128)}, u32[]{:S(2)}) %copy-start.1) | copy-done | bytes 98328
  2.5 0.0 copy-start.2
  2.5 0.9 %copy-done.2 = f32[3,8,8,128]{3,2,1,0:T(8,128)S(1)} copy-done((f32[3,8,8,128]{3,2,1,0:T(8,128)S(1)}, f32[3,8,8,128]{3,2,1,0:T(8,128)}, u32[]{:S(2)}) %copy-start.2) | copy-done | bytes 98328
  3.4 0.0 copy-start.3
  3.4 0.9 %copy-done.3 = f32[3,8,8,128]{3,2,1,0:T(8,128)S(1)} copy-done((f32[3,8,8,128]{3,2,1,0:T(8,128)S(1)}, f32[3,8,8,128]{3,2,1,0:T(8,128)}, u32[]{:S(2)}) %copy-start.3) | copy-done | bytes 98328
  4.3 40.1 %shard_map.75 = (f32[3,8,8,128]{3,2,1,0:T(8,128)S(1)}, f32[3,8,8,128]{3,2,1,0:T(8,128)S(1)}, f32[3,8,8,128]{3,2,1,0:T(8,128)S(1)}, f32[1,1]{1,0:T(1,128)}) custom-call(f32[3,8,8,128]{3,2,1,0:T(8,128)S(1)} %copy-done.1, f32[3,8,8,128]{3,2,1,0:T(8,128)S(1)} %copy-done.2, f32[3,8,8,128]{3,2,1,0:T(8,128)S(1)} %copy-done.3, s32[12,8,8,128]{3,2,1,0:T(8,128)S(1)} %copy-done), custom_call_target="tpu_custom_call" | custom-call | tf_op jit(solution)/shard_map/pallas_call | solution.py:451
  44.5 0.6 %copy.12 = f32[3,8,8,128]{3,2,1,0:T(8,128)} copy(f32[3,8,8,128]{3,2,1,0:T(8,128)S(1)} %get-tuple-element.16) | data formatting | bytes 196608
  45.1 0.6 %copy.13 = f32[3,8,8,128]{3,2,1,0:T(8,128)} copy(f32[3,8,8,128]{3,2,1,0:T(8,128)S(1)} %get-tuple-element.17) | data formatting | bytes 196608
  45.7 0.6 %copy.14 = f32[3,8,8,128]{3,2,1,0:T(8,128)} copy(f32[3,8,8,128]{3,2,1,0:T(8,128)S(1)} %get-tuple-element.18) | data formatting | bytes 196608
Async XLA Ops:
  0.6 1.0 %copy-start = (s32[12,8,8,128]{3,2,1,0:T(8,128)S(1)}, s32[12,8,8,128]{3,2,1,0:T(8,128)}, u32[]{:S(2)}) copy-start(s32[12,8,8,128]{3,2,1,0:T(8,128)} %broken_hbm.1) | copy-start | bytes 1179652
  1.6 0.9 %copy-start.1 = (f32[3,8,8,128]{3,2,1,0:T(8,128)S(1)}, f32[3,8,8,128]{3,2,1,0:T(8,128)}, u32[]{:S(2)}) copy-start(f32[3,8,8,128]{3,2,1,0:T(8,128)} %disp_hbm.1) | copy-start | bytes 294916
  2.5 0.9 %copy-start.2 = (f32[3,8,8,128]{3,2,1,0:T(8,128)S(1)}, f32[3,8,8,128]{3,2,1,0:T(8,128)}, u32[]{:S(2)}) copy-start(f32[3,8,8,128]{3,2,1,0:T(8,128)} %vel_hbm.1) | copy-start | bytes 294916
  3.4 0.9 %copy-start.3 = (f32[3,8,8,128]{3,2,1,0:T(8,128)S(1)}, f32[3,8,8,128]{3,2,1,0:T(8,128)}, u32[]{:S(2)}) copy-start(f32[3,8,8,128]{3,2,1,0:T(8,128)} %body_hbm.1) | copy-start | bytes 294916

commit v2 on v1

--- a/solution.py
+++ b/solution.py
@@ -99,13 +99,13 @@
 
 
 def step_kernel(
-    counts, depth_total, area,
+    counts, depth_total, area, direct,
     disp_hbm, vel_hbm, body_hbm, broken_hbm,
-    new_disp_ref, new_vel_ref, new_acc_ref, energy_ref,
-    disp_ref, vel_ref, body_ref, broken_ref, acc_ref,
+    acc_ref, force_ref, energy_ref,
+    disp_ref, vel_ref, body_ref, broken_ref, new_disp_ref,
     e1_ref, e2_ref, mask_ref, outside_ref,
     slab_ref, pack_ref, own_z, own_0, far_z, far_0, far_x,
-    slot_x, slot_y, slot_z, etile_ref,
+    slots, etile_ref,
     in_sem, recv_sem, send_sem, esend_sem, erecv_sem,
 ):
     nx, ny, nz = counts
@@ -169,7 +169,7 @@
                 else:
                     pl.when(has_z[dz])(greet)
                     maybe[dz] += 1
-    for axis, count, me in zip(AXES, counts, (ix, iy, iz)):
+    for axis, count, me in zip(AXES, counts, (ix, iy, iz)) if not direct else ():
         for d in range(1, count):
             pl.semaphore_signal(
                 barrier, inc=1, device_id={axis: lax.rem(me + d, count)}, device_id_type=MESH
@@ -336,7 +336,7 @@
     inputs[2].wait()
     inputs[3].wait()
     acc_ref[...] = body_ref[...]
-    new_acc_ref[...] = body_ref[...]
+    force_ref[...] = jnp.zeros_like(force_ref)
     etile_ref[...] = jnp.zeros_like(etile_ref)
 
     for g in (HIGH, LOW):
@@ -361,7 +361,6 @@
             new_disp_ref[c, x] = (
                 disp_ref[c, x] + TIME_STEP * v + 0.5 * TIME_STEP * TIME_STEP * a
             )
-            new_vel_ref[c, x] = v + 0.5 * TIME_STEP * a
 
         @pl.when(i == rows - W - 1)
         def _():
@@ -398,37 +397,58 @@
         energy = jnp.zeros(etile_ref.shape, jnp.float32)
         for p in REACH:
             x = lax.rem(j + (W - p + rows), rows)
-            energy = row_bonds(p, x, e2_ref, mask_ref, new_acc_ref, depth, energy)
+            energy = row_bonds(p, x, e2_ref, mask_ref, force_ref, depth, energy)
         etile_ref[...] += energy
         return carry
 
     lax.fori_loop(0, rows, second, 0)
-    for c in range(3):
-        for x in range(rows):
-            new_vel_ref[c, x] = new_vel_ref[c, x] + 0.5 * TIME_STEP * new_acc_ref[c, x]
-
-    at = 0
-    value = etile_ref[...]
-    for slot, axis, count, me in zip((slot_x, slot_y, slot_z), AXES, counts, (ix, iy, iz)):
-        slot[me] = value
-        moves = []
-        for d in range(1, count):
+    moves = []
+    if direct:
+        me = (ix * ny + iy) * nz + iz
+        slots[me] = jnp.sum(etile_ref[...], axis=0, keepdims=True)
+        for d in range(1, nx * ny * nz):
+            dx, dy, dz = d // (ny * nz), d // nz % ny, d % nz
             copy = pltpu.make_async_remote_copy(
-                src_ref=slot.at[me],
-                dst_ref=slot.at[me],
-                send_sem=esend_sem.at[at],
-                recv_sem=erecv_sem.at[at],
-                device_id={axis: lax.rem(me + d, count)},
+                src_ref=slots.at[me],
+                dst_ref=slots.at[me],
+                send_sem=esend_sem.at[d],
+                recv_sem=erecv_sem.at[d],
+                device_id={
+                    "gx": lax.rem(ix + dx, nx),
+                    "gy": lax.rem(iy + dy, ny),
+                    "gz": lax.rem(iz + dz, nz),
+                },
                 device_id_type=MESH,
             )
             copy.start()
             moves.append(copy)
-            at += 1
         for copy in moves:
             copy.wait()
-        value = slot[0]
-        for i in range(1, count):
-            value = value + slot[i]
+        value = slots[...]
+    else:
+        value = jnp.sum(etile_ref[...], axis=0, keepdims=True)
+        at = 0
+        for axis, count, me in zip(AXES, counts, (ix, iy, iz)):
+            base = at + AXES.index(axis)
+            slots[base + me] = value
+            moves = []
+            for d in range(1, count):
+                copy = pltpu.make_async_remote_copy(
+                    src_ref=slots.at[base + me],
+                    dst_ref=slots.at[base + me],
+                    send_sem=esend_sem.at[at],
+                    recv_sem=erecv_sem.at[at],
+                    device_id={axis: lax.rem(me + d, count)},
+                    device_id_type=MESH,
+                )
+                copy.start()
+                moves.append(copy)
+                at += 1
+            for copy in moves:
+                copy.wait()
+            value = slots[base]
+            for i in range(1, count):
+                value = value + slots[base + i]
     energy_ref[0, 0] = jnp.sum(value) * jnp.float32(1.0 / area)
 
     for ex, src in ((0, disp_ref), (1, new_disp_ref)):
@@ -443,16 +463,18 @@
     padded = align(depth + 2 * W)
     slab = align(9 * (rows - W))
     far = align(9 * W)
-    peers = sum(counts) - len(counts)
+    devices = math.prod(counts)
+    direct = devices if devices <= 64 else 0
+    peers = max(direct, sum(counts))
     block = pltpu.VMEM((3, rows, depth, width), jnp.float32)
     out = jax.ShapeDtypeStruct((3, rows, depth, width), jnp.float32)
     vmem = pl.BlockSpec(memory_space=pltpu.VMEM)
     e_shape = pltpu.VMEM((2 * W + 1, 3, rows + 2 * W, padded, width), jnp.float32)
-    new_disp, new_vel, new_acc, energy = pl.pallas_call(
-        functools.partial(step_kernel, counts, depth * counts[2], area),
-        out_shape=(out, out, out, jax.ShapeDtypeStruct((1, 1), jnp.float32)),
-        in_specs=[pl.BlockSpec(memory_space=pl.ANY)] * 4,
-        out_specs=(vmem, vmem, vmem, pl.BlockSpec(memory_space=pltpu.SMEM)),
+    acc, force, energy = pl.pallas_call(
+        functools.partial(step_kernel, counts, depth * counts[2], area, direct),
+        out_shape=(out, out, jax.ShapeDtypeStruct((1, 1), jnp.float32)),
+        in_specs=[pl.BlockSpec(memory_space=pltpu.HBM)] * 4,
+        out_specs=(vmem, vmem, pl.BlockSpec(memory_space=pltpu.SMEM)),
         scratch_shapes=[
             block, block, block,
             pltpu.VMEM((broken.shape[0], rows, depth, width), jnp.int32),
@@ -468,8 +490,8 @@
             pltpu.VMEM((2, 2, 16, width), jnp.float32),
             pltpu.VMEM((2, 2, 3, W, depth, width), jnp.float32),
         ]
-        + [pltpu.VMEM((count, depth, width), jnp.float32) for count in counts]
         + [
+            pltpu.VMEM((max(direct, sum(counts)), 1, width), jnp.float32),
             pltpu.VMEM((depth, width), jnp.float32),
             pltpu.SemaphoreType.DMA((4,)),
             pltpu.SemaphoreType.DMA((2, 2, 7)),
@@ -478,10 +500,15 @@
             pltpu.SemaphoreType.DMA((peers,)),
         ],
         compiler_params=pltpu.CompilerParams(
-            collective_id=0, has_side_effects=True, vmem_limit_bytes=48 * 1024 * 1024
+            collective_id=0, has_side_effects=True, vmem_limit_bytes=67043328
         ),
     )(displacement, velocity, body_force, broken)
-    return new_disp, new_vel, new_acc, energy.reshape(())
+    new_displacement = (
+        displacement + TIME_STEP * velocity + 0.5 * TIME_STEP * TIME_STEP * acc
+    )
+    new_acceleration = force + body_force
+    new_velocity = velocity + 0.5 * TIME_STEP * (acc + new_acceleration)
+    return new_displacement, new_velocity, new_acceleration, energy.reshape(())
 
 
 def solution(mesh):

time: 48.4 us -> 40.2 us (0.83)
  local copies, waits for them, and re-layouts: 5.59 us -> 0 us
  Pallas kernels: 40.1 us -> 35.9 us
  other arithmetic: 0 us -> 1.81 us
    unnamed x11 -> x0, local copies, waits for them, and re-layouts: 5.59 us -> none
    pallas_call x1, Pallas kernels: 40.1 us -> 35.9 us  [per_device(): pl.pallas_call(functools.partial(step_kernel, counts, depth * counts[2],...]
    add x0 -> x1, other arithmetic: none -> 1.81 us  [per_device(): new_velocity = velocity + 0.5 * TIME_STEP * (acc + new_acceleration)]
where the time goes in v2:
time: 40.2 us; the launch traced here: 40 us
  Pallas kernels  35.9 us (89%)
  between operations  2.33 us (6%)
  other arithmetic  1.81 us (5%)
    pallas_call x1, Pallas kernels, per_device(): pl.pallas_call(functools.partial(step_kernel, counts, depth * counts[2],...  35.9 us
    add x1, other arithmetic, per_device(): new_velocity = velocity + 0.5 * TIME_STEP * (acc + new_acceleration)  1.81 us

profile of v2, /device:TPU:0, one launch (start us, length us, event | category | flops | bytes accessed | tf_op | source)
XLA Modules:
  0.0 40.0 jit_solution(14965442169810686533)
XLA Ops:
  0.6 35.9 %shard_map.75 = (f32[3,8,8,128]{3,2,1,0:T(8,128)}, f32[3,8,8,128]{3,2,1,0:T(8,128)}, f32[1,1]{1,0:T(1,128)}) custom-call(f32[3,8,8,128]{3,2,1,0:T(8,128)} %disp_hbm.1, f32[3,8,8,128]{3,2,1,0:T(8,128)} %vel_hbm.1, f32[3,8,8,128]{3,2,1,0:T(8,128)} %body_hbm.1, s32[12,8,8,128]{3,2,1,0:T(8,128)} %broken_hbm.1), custom_call_target="tpu_custom_call" | custom-call | tf_op jit(solution)/shard_map/pallas_call | solution.py:473
  36.5 1.8 %multiply_add_fusion = (f32[3,8,8,128]{3,2,1,0:T(8,128)}, f32[3,8,8,128]{3,2,1,0:T(8,128)}, f32[3,8,8,128]{3,2,1,0:T(8,128)}) fusion(f32[3,8,8,128]{3,2,1,0:T(8,128)} %vel_hbm.1, f32[3,8,8,128]{3,2,1,0:T(8,128)} %get-tuple-element.7, f32[3,8,8,128]{3,2,1,0:T(8,128)} %get-tuple-element.8, f32[3,8,8,128]{3,2,1,0:T(8,128)} %body_hbm.1, f32[3,8,8,128]{3,2,1,0:T(8,128)} %disp_hbm.1), kind=kLoop, calls=%fused_computation | loop fusion | flops 196608 | bytes 786432 | tf_op jit(solution)/shard_map/add | solution.py:510

commit v3 on v2

--- a/solution.py
+++ b/solution.py
@@ -53,57 +53,84 @@
     def body(x, carry):
         for w in range(WORD_COUNT):
             word = broken_ref[w, x] | outside_ref[w]
+            turned = {r: rotated(word, r) for r in REACH}
             for k in range(w * BITS_PER_WORD, min(len(BONDS), (w + 1) * BITS_PER_WORD)):
                 p, q, r = BONDS[k]
                 weight = MICRO_MODULUS * math.exp(-(p * p + q * q + r * r) / 9.0)
-                bit = word & (1 << (k % BITS_PER_WORD))
+                bit = turned[r] & (1 << (k % BITS_PER_WORD))
                 mask_ref[k, x] = jnp.where(bit == 0, jnp.float32(weight), jnp.float32(0.0))
         return carry
 
     lax.fori_loop(0, rows, body, 0)
 
 
-def row_bonds(p, x, e_ref, mask_ref, acc_ref, depth, energy):
-    center = [e_ref[W, c, x + W, W : W + depth] for c in range(3)]
-    force = [acc_ref[c, x] for c in range(3)]
+def rotated(tile, r):
+    width = tile.shape[1]
+    return pltpu.roll(tile, r % width, 1) if r else tile
+
+
+def bond(p, q, r, x, center_x, center, e_ref, mask_ref):
+    rest = math.sqrt(p * p + q * q + r * r)
+    bx = e_ref[r + W, q + W, 0, x + (W + p)] - center_x
+    bz = e_ref[r + W, q + W, 1, x + (W + p)] - center[1]
+    by = e_ref[r + W, q + W, 2, x + (W + p)] - center[2]
+    square = bx * bx + bz * bz + by * by
+    h = jnp.float32(1.0 / rest) - lax.rsqrt(square)
+    return (bx, bz, by), square, h, mask_ref[INDEX[p, q, r], x] * h
+
+
+def line_force(p, r, x, center, force, e_ref, mask_ref):
     center_x = center[0] - float(p)
-    center_z = {q: center[1] - float(q) for q in REACH}
-    classes = {}
     for q in REACH:
-        for r in REACH:
-            if (p, q, r) != (0, 0, 0):
-                key = 0 if energy is None else q * q + r * r
-                classes.setdefault(key, []).append((q, r))
-    for key in sorted(classes):
-        part = None
-        for q, r in classes[key]:
-            rest = math.sqrt(p * p + q * q + r * r)
-            nb = [e_ref[r + W, c, x + (W + p), W + q : W + q + depth] for c in range(3)]
-            bx = nb[0] - center_x
-            bz = nb[1] - center_z[q]
-            by = nb[2] - center[2]
-            square = bx * bx + bz * bz + by * by
-            h = jnp.float32(1.0 / rest) - lax.rsqrt(square)
-            g = mask_ref[INDEX[p, q, r], x] * h
-            force[0] = force[0] + g * bx
-            force[1] = force[1] + g * bz
-            force[2] = force[2] + g * by
-            if energy is not None:
-                e = g * (h * square)
-                part = e if part is None else part + e
-        if energy is not None:
-            energy = energy + part * jnp.float32(0.25 * rest)
-    for c in range(3):
-        acc_ref[c, x] = force[c]
-    return energy
+        if (p, q, r) != (0, 0, 0):
+            b, _, _, g = bond(p, q, r, x, center_x, center, e_ref, mask_ref)
+            force = [f + g * d for f, d in zip(force, b)]
+    return force
+
+
+def line_energy(p, r, x, center, e_ref, mask_ref, parts):
+    center_x = center[0] - float(p)
+    for q in REACH:
+        if (p, q, r) != (0, 0, 0):
+            _, square, h, g = bond(p, q, r, x, center_x, center, e_ref, mask_ref)
+            mask_ref[INDEX[p, q, r], x] = g
+            e = g * (h * square)
+            key = q * q + r * r
+            parts[key] = parts[key] + e if key in parts else e
+
+
+def tree_sum(terms):
+    terms = list(terms)
+    while len(terms) > 1:
+        pairs = [a + b for a, b in zip(terms[::2], terms[1::2])]
+        terms = pairs + terms[len(pairs) * 2 :]
+    return terms[0]
+
+
+def kept_force(r, x, center, e_ref, g_ref):
+    lines = []
+    for p in REACH:
+        kept = [q for q in REACH if (p, q, r) != (0, 0, 0)]
+        g = [g_ref[INDEX[p, q, r], x] for q in kept]
+        count = tree_sum(g)
+        line = [
+            tree_sum([a * e_ref[r + W, q + W, c, x + (W + p)] for a, q in zip(g, kept)])
+            for c in range(3)
+        ]
+        if p:
+            line[0] = line[0] + float(p) * count
+        lines.append(line + [count])
+    *force, total = (tree_sum(part) for part in zip(*lines))
+    return [f - c * total for f, c in zip(force, center)]
 
 
 def step_kernel(
     counts, depth_total, area, direct,
     disp_hbm, vel_hbm, body_hbm, broken_hbm,
-    acc_ref, force_ref, energy_ref,
-    disp_ref, vel_ref, body_ref, broken_ref, new_disp_ref,
-    e1_ref, e2_ref, mask_ref, outside_ref,
+    acc_hbm, force_hbm, energy_ref,
+    disp_ref, vel_ref, body_ref, broken_ref, new_disp_ref, acc_ref, force_ref,
+    e1_ref, e2_ref, c1_ref, c2_ref, ext_ref, side_ref, edge_ref,
+    mask_ref, outside_ref,
     slab_ref, pack_ref, own_z, own_0, far_z, far_0, far_x,
     slots, etile_ref,
     in_sem, recv_sem, send_sem, esend_sem, erecv_sem,
@@ -267,57 +294,65 @@
                 functools.partial(arrived, far_z.at[ex, g, s, 0 : far_rows + 16], ex, g, 3 + s)
             )
 
-    padded = e1_ref.shape[3]
-    wide = lax.broadcasted_iota(jnp.int32, (padded, width), 1)
-
-    def fill(e_ref, ex, g, k, row, far, src):
+    below_w = lane < 0
+    for t in range(width // (2 * W)):
+        below_w = below_w | ((lane >= 2 * W * t) & (lane < 2 * W * t + W))
+
+    def combine(ex, g, far):
         z_ref, zero_ref = (far_z, far_0) if far else (own_z, own_0)
         n = far_rows if far else slab_rows[g]
-        edges = []
-        for i in range(2):
-            below = z_ref[ex, g, 0, n + 8 * i : n + 8 * i + 8]
-            here = zero_ref[ex, g, 8 * i : 8 * i + 8]
-            above = z_ref[ex, g, 1, n + 8 * i : n + 8 * i + 8]
-            spare = jnp.zeros((padded - depth - 2 * W, width), jnp.float32)
-            edges.append(
-                jnp.concatenate([below[depth - W :], here, above[:W], spare], axis=0)
-            )
+        at = 2 * g + far
+
+        def both(ref, *where):
+            return jnp.where(
+                below_w, ref[(*where, slice(0, 8))], ref[(*where, slice(8, 16))]
+            )
+
+        edge_ref[at, 0:W] = both(z_ref.at[ex, g, 0, n : n + 16])[depth - W :]
+        edge_ref[at, W : W + depth] = both(zero_ref.at[ex, g])
+        edge_ref[at, W + depth : 2 * W + depth] = both(z_ref.at[ex, g, 1, n : n + 16])[:W]
+        return edge_ref[at]
+
+    def fill(e_ref, ex, g, k, row, far, edge, src):
+        z_ref = far_z if far else own_z
         for c in range(3):
             at = 9 * k + 3 * c
-            tile = jnp.concatenate(
-                [
-                    z_ref[ex, g, 0, at : at + W],
-                    src(c),
-                    z_ref[ex, g, 1, at : at + W],
-                    jnp.zeros((padded - depth - 2 * W, width), jnp.float32),
-                ],
-                axis=0,
-            )
-            at = 6 * (3 * k + c)
-            side = jnp.where(
-                wide < W,
-                pltpu.roll(edges[1], (2 * width - at - W) % width, 1),
-                pltpu.roll(edges[0], (2 * width - W - at) % width, 1),
-            )
-            for r in REACH:
-                if r == 0:
-                    moved = tile
-                elif r > 0:
-                    moved = pltpu.roll(jnp.where(wide < r, side, tile), width - r, 1)
-                else:
-                    moved = pltpu.roll(jnp.where(wide >= width + r, side, tile), -r, 1)
-                if c == 2 and r != 0:
-                    moved = moved + float(r)
-                e_ref[r + W, c, row] = moved
+            ext_ref[c, row, 0:W] = z_ref[ex, g, 0, at : at + W]
+            ext_ref[c, row, W : W + depth] = src(c)
+            ext_ref[c, row, W + depth : 2 * W + depth] = z_ref[ex, g, 1, at : at + W]
+            at = 2 * W * (3 * k + c)
+            side_ref[c, row] = pltpu.roll(edge, (2 * width - W - at) % width, 1)
+            for q in REACH:
+                tile = ext_ref[c, row, W + q : W + q + depth]
+                side = side_ref[c, row, W + q : W + q + depth]
+                if c == 1 and q:
+                    tile, side = tile + float(q), side + float(q)
+                for r in REACH:
+                    if r == 0:
+                        value = tile
+                    elif r > 0:
+                        value = jnp.where(lane < r, side, tile)
+                    else:
+                        value = jnp.where(lane >= width + r, side, tile)
+                    if c == 2 and r:
+                        value = value + float(r)
+                    e_ref[r + W, q + W, c, row] = value
 
     def fill_own(e_ref, ex, g, src):
+        edge = combine(ex, g, 0)
         for k, x in enumerate(group_rows[g]):
-            fill(e_ref, ex, g, k, x + W, False, lambda c, x=x: src[c, x])
+            fill(e_ref, ex, g, k, x + W, 0, edge, lambda c, x=x: src[c, x])
 
     def fill_far(e_ref, ex, g):
+        edge = combine(ex, g, 1)
         for k in range(W):
             row = k if g == HIGH else rows + W + k
-            fill(e_ref, ex, g, k, row, True, lambda c, k=k: far_x[ex, g, c, k])
+            fill(e_ref, ex, g, k, row, 1, edge, lambda c, k=k: far_x[ex, g, c, k])
+
+    def turn(c_ref, x, src):
+        for c in range(3):
+            for r in REACH:
+                c_ref[r + W, c, x] = rotated(src[c, x], r)
 
     inputs[0].wait()
     for g in (HIGH, LOW):
@@ -337,6 +372,8 @@
     inputs[3].wait()
     acc_ref[...] = body_ref[...]
     force_ref[...] = jnp.zeros_like(force_ref)
+    for x in range(rows):
+        turn(c1_ref, x, disp_ref)
     etile_ref[...] = jnp.zeros_like(etile_ref)
 
     for g in (HIGH, LOW):
@@ -353,8 +390,14 @@
                 fill_far(e1_ref, 0, g)
 
         x = lax.rem(i + W, rows)
-        for p in REACH:
-            row_bonds(p, x, e1_ref, mask_ref, acc_ref, depth, None)
+        turn(c2_ref, lax.rem(i + (W - 1), rows), new_disp_ref)
+        for r in REACH:
+            center = [c1_ref[r + W, c, x] for c in range(3)]
+            force = [jnp.zeros((depth, width), jnp.float32)] * 3
+            for p in REACH:
+                force = line_force(p, r, x, center, force, e1_ref, mask_ref)
+            for c in range(3):
+                acc_ref[c, x] += rotated(force[c], -r)
         for c in range(3):
             a = acc_ref[c, x]
             v = vel_ref[c, x]
@@ -370,6 +413,7 @@
         return carry
 
     lax.fori_loop(0, rows, first, 0)
+    turn(c2_ref, W - 1, new_disp_ref)
     stage(1, LOW, new_disp_ref)
     each(copies(1, LOW, new_disp_ref), lambda copy: copy.start())
 
@@ -378,9 +422,6 @@
         def _():
             wait_own(1, HIGH)
             fill_own(e2_ref, 1, HIGH, new_disp_ref)
-            for c in range(3):
-                for x in range(W):
-                    e2_ref[W, c, x + W, W : W + depth] = new_disp_ref[c, x]
 
         @pl.when(j == rows - 2 * W)
         def _():
@@ -397,11 +438,37 @@
         energy = jnp.zeros(etile_ref.shape, jnp.float32)
         for p in REACH:
             x = lax.rem(j + (W - p + rows), rows)
-            energy = row_bonds(p, x, e2_ref, mask_ref, force_ref, depth, energy)
+            parts = {}
+            for r in REACH:
+                center = [c2_ref[r + W, c, x] for c in range(3)]
+                line_energy(p, r, x, center, e2_ref, mask_ref, parts)
+            for key, part in parts.items():
+                energy = energy + part * jnp.float32(0.25 * math.sqrt(p * p + key))
         etile_ref[...] += energy
         return carry
 
     lax.fori_loop(0, rows, second, 0)
+    def third(x, carry):
+        for r in REACH:
+            center = [c2_ref[r + W, c, x] for c in range(3)]
+            force = kept_force(r, x, center, e2_ref, mask_ref)
+            for c in range(3):
+                force_ref[c, x] += rotated(force[c], -r)
+        return carry
+
+    results = [
+        pltpu.make_async_copy(acc_ref, acc_hbm, in_sem.at[4]),
+        pltpu.make_async_copy(force_ref, force_hbm, in_sem.at[5]),
+    ]
+    results[0].start()
+
+    def sum_force():
+        lax.fori_loop(0, rows, third, 0)
+        results[1].start()
+        for ex, src in ((0, disp_ref), (1, new_disp_ref)):
+            for g in (HIGH, LOW):
+                each(copies(ex, g, src), lambda copy: copy.wait_send())
+
     moves = []
     if direct:
         me = (ix * ny + iy) * nz + iz
@@ -412,7 +479,7 @@
                 src_ref=slots.at[me],
                 dst_ref=slots.at[me],
                 send_sem=esend_sem.at[d],
-                recv_sem=erecv_sem.at[d],
+                recv_sem=erecv_sem.at[0],
                 device_id={
                     "gx": lax.rem(ix + dx, nx),
                     "gy": lax.rem(iy + dy, ny),
@@ -422,10 +489,14 @@
             )
             copy.start()
             moves.append(copy)
+        sum_force()
         for copy in moves:
-            copy.wait()
+            copy.wait_send()
+        landed = slots.at[: nx * ny * nz - 1]
+        pltpu.make_async_copy(landed, landed, erecv_sem.at[0]).wait()
         value = slots[...]
     else:
+        sum_force()
         value = jnp.sum(etile_ref[...], axis=0, keepdims=True)
         at = 0
         for axis, count, me in zip(AXES, counts, (ix, iy, iz)):
@@ -451,9 +522,8 @@
                 value = value + slots[base + i]
     energy_ref[0, 0] = jnp.sum(value) * jnp.float32(1.0 / area)
 
-    for ex, src in ((0, disp_ref), (1, new_disp_ref)):
-        for g in (HIGH, LOW):
-            each(copies(ex, g, src), lambda copy: copy.wait_send())
+    for copy in results:
+        copy.wait()
 
 
 def per_device(displacement, velocity, body_force, broken):
@@ -468,18 +538,22 @@
     peers = max(direct, sum(counts))
     block = pltpu.VMEM((3, rows, depth, width), jnp.float32)
     out = jax.ShapeDtypeStruct((3, rows, depth, width), jnp.float32)
-    vmem = pl.BlockSpec(memory_space=pltpu.VMEM)
-    e_shape = pltpu.VMEM((2 * W + 1, 3, rows + 2 * W, padded, width), jnp.float32)
+    hbm = pl.BlockSpec(memory_space=pltpu.HBM)
+    span = 2 * W + 1
+    e_shape = pltpu.VMEM((span, span, 3, rows + 2 * W, depth, width), jnp.float32)
+    turned = pltpu.VMEM((span, 3, rows, depth, width), jnp.float32)
+    halo = pltpu.VMEM((3, rows + 2 * W, padded, width), jnp.float32)
     acc, force, energy = pl.pallas_call(
         functools.partial(step_kernel, counts, depth * counts[2], area, direct),
         out_shape=(out, out, jax.ShapeDtypeStruct((1, 1), jnp.float32)),
-        in_specs=[pl.BlockSpec(memory_space=pltpu.HBM)] * 4,
-        out_specs=(vmem, vmem, pl.BlockSpec(memory_space=pltpu.SMEM)),
+        in_specs=[hbm] * 4,
+        out_specs=(hbm, hbm, pl.BlockSpec(memory_space=pltpu.SMEM)),
         scratch_shapes=[
             block, block, block,
             pltpu.VMEM((broken.shape[0], rows, depth, width), jnp.int32),
-            block,
-            e_shape, e_shape,
+            block, block, block,
+            e_shape, e_shape, turned, turned, halo, halo,
+            pltpu.VMEM((4, padded, width), jnp.float32),
             pltpu.VMEM((len(BONDS), rows, depth, width), jnp.float32),
             pltpu.VMEM((WORD_COUNT, depth, width), jnp.int32),
             pltpu.VMEM((2, 2, 2, slab, width), jnp.float32),
@@ -493,7 +567,7 @@
         + [
             pltpu.VMEM((max(direct, sum(counts)), 1, width), jnp.float32),
             pltpu.VMEM((depth, width), jnp.float32),
-            pltpu.SemaphoreType.DMA((4,)),
+            pltpu.SemaphoreType.DMA((6,)),
             pltpu.SemaphoreType.DMA((2, 2, 7)),
             pltpu.SemaphoreType.DMA((2, 2, 17)),
             pltpu.SemaphoreType.DMA((peers,)),

time: 40.2 us -> 36.7 us (0.913)
  Pallas kernels: 35.9 us -> 32.3 us
    pallas_call x1, Pallas kernels: 35.9 us -> 32.3 us  [per_device(): pl.pallas_call(functools.partial(step_kernel, counts, depth * counts[2],...]
where the time goes in v3:
time: 36.7 us; the launch traced here: 36.5 us
  Pallas kernels  32.3 us (88%)
  between operations  2.33 us (6%)
  other arithmetic  1.81 us (5%)
    pallas_call x1, Pallas kernels, per_device(): pl.pallas_call(functools.partial(step_kernel, counts, depth * counts[2],...  32.3 us
    add x1, other arithmetic, per_device(): new_velocity = velocity + 0.5 * TIME_STEP * (acc + new_acceleration)  1.81 us

profile of v3, /device:TPU:0, one launch (start us, length us, event | category | flops | bytes accessed | tf_op | source)
XLA Modules:
  0.0 36.5 jit_solution(4401601615379796409)
XLA Ops:
  0.6 32.3 %shard_map.75 = (f32[3,8,8,128]{3,2,1,0:T(8,128)}, f32[3,8,8,128]{3,2,1,0:T(8,128)}, f32[1,1]{1,0:T(1,128)}) custom-call(f32[3,8,8,128]{3,2,1,0:T(8,128)} %disp_hbm.1, f32[3,8,8,128]{3,2,1,0:T(8,128)} %vel_hbm.1, f32[3,8,8,128]{3,2,1,0:T(8,128)} %body_hbm.1, s32[12,8,8,128]{3,2,1,0:T(8,128)} %broken_hbm.1), custom_call_target="tpu_custom_call" | custom-call | tf_op jit(solution)/shard_map/pallas_call | solution.py:546
  33.0 1.8 %multiply_add_fusion = (f32[3,8,8,128]{3,2,1,0:T(8,128)}, f32[3,8,8,128]{3,2,1,0:T(8,128)}, f32[3,8,8,128]{3,2,1,0:T(8,128)}) fusion(f32[3,8,8,128]{3,2,1,0:T(8,128)} %vel_hbm.1, f32[3,8,8,128]{3,2,1,0:T(8,128)} %get-tuple-element.7, f32[3,8,8,128]{3,2,1,0:T(8,128)} %get-tuple-element.8, f32[3,8,8,128]{3,2,1,0:T(8,128)} %body_hbm.1, f32[3,8,8,128]{3,2,1,0:T(8,128)} %disp_hbm.1), kind=kLoop, calls=%fused_computation | loop fusion | flops 196608 | bytes 786432 | tf_op jit(solution)/shard_map/add | solution.py:584

commit v4 on v3

--- a/solution.py
+++ b/solution.py
@@ -45,20 +45,66 @@
     return words
 
 
+def signed(bits):
+    return bits - (1 << 32) if bits >> 31 else bits
+
+
+def turned_bits(words):
+    out = {}
+    for r in REACH:
+        taken = {}
+        for (p, q, r2), k in INDEX.items():
+            if r2 == r:
+                taken.setdefault(k // BITS_PER_WORD, []).append(k)
+        if r == 0:
+            for w, ks in taken.items():
+                for k in ks:
+                    out[k] = (words[w], signed(1 << (k % BITS_PER_WORD)))
+            continue
+        packs = []
+        for w, ks in taken.items():
+            at = sum(1 << (k % BITS_PER_WORD) for k in ks)
+            shifts = sorted(range(-BITS_PER_WORD, BITS_PER_WORD), key=abs)
+            home = None
+            for pack in packs:
+                for shift in shifts:
+                    moved = at << shift if shift >= 0 else at >> -shift
+                    whole = (moved >> shift if shift >= 0 else moved << -shift) == at
+                    if whole and moved < 1 << 32 and not moved & pack[0]:
+                        home = (pack, shift, moved)
+                        break
+                if home:
+                    break
+            if home is None:
+                packs.append([0, None, []])
+                home = (packs[-1], 0, at)
+            pack, shift, moved = home
+            value = words[w] & at
+            if shift > 0:
+                value = value << shift
+            elif shift < 0:
+                value = value >> -shift
+            pack[0] |= moved
+            pack[1] = value if pack[1] is None else pack[1] | value
+            pack[2] += [(k, k % BITS_PER_WORD + shift) for k in ks]
+        for _, value, bonds in packs:
+            value = rotated(value, r)
+            for k, at in bonds:
+                out[k] = (value, signed(1 << at))
+    return out
+
+
 def store_masks(broken_ref, mask_ref, outside_ref, depth_start, depth_total):
     rows = broken_ref.shape[1]
     for w, word in enumerate(depth_bits(broken_ref.shape[2:], depth_start, depth_total)):
         outside_ref[w] = word
 
     def body(x, carry):
-        for w in range(WORD_COUNT):
-            word = broken_ref[w, x] | outside_ref[w]
-            turned = {r: rotated(word, r) for r in REACH}
-            for k in range(w * BITS_PER_WORD, min(len(BONDS), (w + 1) * BITS_PER_WORD)):
-                p, q, r = BONDS[k]
-                weight = MICRO_MODULUS * math.exp(-(p * p + q * q + r * r) / 9.0)
-                bit = turned[r] & (1 << (k % BITS_PER_WORD))
-                mask_ref[k, x] = jnp.where(bit == 0, jnp.float32(weight), jnp.float32(0.0))
+        words = [broken_ref[w, x] | outside_ref[w] for w in range(WORD_COUNT)]
+        for k, (tile, bit) in turned_bits(words).items():
+            p, q, r = BONDS[k]
+            weight = MICRO_MODULUS * math.exp(-(p * p + q * q + r * r) / 9.0)
+            mask_ref[k, x] = jnp.where(tile & bit == 0, jnp.float32(weight), jnp.float32(0.0))
         return carry
 
     lax.fori_loop(0, rows, body, 0)
@@ -107,9 +153,9 @@
     return terms[0]
 
 
-def kept_force(r, x, center, e_ref, g_ref):
+def kept_force(r, steps, x, center, e_ref, g_ref):
     lines = []
-    for p in REACH:
+    for p in steps:
         kept = [q for q in REACH if (p, q, r) != (0, 0, 0)]
         g = [g_ref[INDEX[p, q, r], x] for q in kept]
         count = tree_sum(g)
@@ -228,7 +274,7 @@
                     pltpu.make_async_remote_copy(
                         src_ref=src_ref,
                         dst_ref=dst_ref,
-                        send_sem=send_sem.at[ex, g, len(out)],
+                        send_sem=send_sem.at[ex, g, dz + 1],
                         recv_sem=recv_sem.at[ex, g, kind],
                         device_id=device(dx, dy, dz),
                         device_id_type=MESH,
@@ -276,6 +322,16 @@
 
     def arrived(ref, ex, g, kind):
         pltpu.make_async_copy(ref, ref, recv_sem.at[ex, g, kind]).wait()
+
+    def wait_sent(ex, g):
+        def sent(dz, tiles):
+            ref = mask_ref.at[0:tiles, 0]
+            pltpu.make_async_copy(ref, ref, send_sem.at[ex, g, dz + 1]).wait()
+
+        sent(0, 4 + 3 * W)
+        for dz in SIDES:
+            tiles = (slab_rows[g] + far_rows) // 8 + 4
+            pl.when(has_z[dz])(functools.partial(sent, dz, tiles))
 
     def wait_own(ex, g):
         arrived(own_0.at[ex, g], ex, g, 2)
@@ -363,8 +419,10 @@
         expected = expected + jnp.where(has_z[dz], maybe[dz], 0)
     pl.semaphore_wait(barrier, expected)
 
-    for g in (HIGH, LOW):
-        each(copies(0, g, disp_ref), lambda copy: copy.start())
+    pairs = {g: copies(0, g, disp_ref) for g in (HIGH, LOW)}
+    for part in (slice(0, 8), slice(8, None)):
+        for g in (HIGH, LOW):
+            each(pairs[g][part], lambda copy: copy.start())
 
     inputs[1].wait()
     store_masks(broken_ref, mask_ref, outside_ref, iz * depth, depth_total)
@@ -393,11 +451,12 @@
         turn(c2_ref, lax.rem(i + (W - 1), rows), new_disp_ref)
         for r in REACH:
             center = [c1_ref[r + W, c, x] for c in range(3)]
-            force = [jnp.zeros((depth, width), jnp.float32)] * 3
-            for p in REACH:
-                force = line_force(p, r, x, center, force, e1_ref, mask_ref)
-            for c in range(3):
-                acc_ref[c, x] += rotated(force[c], -r)
+            for steps in (REACH[:W], REACH[W:]):
+                force = [jnp.zeros((depth, width), jnp.float32)] * 3
+                for p in steps:
+                    force = line_force(p, r, x, center, force, e1_ref, mask_ref)
+                for c in range(3):
+                    acc_ref[c, x] += rotated(force[c], -r)
         for c in range(3):
             a = acc_ref[c, x]
             v = vel_ref[c, x]
@@ -451,9 +510,10 @@
     def third(x, carry):
         for r in REACH:
             center = [c2_ref[r + W, c, x] for c in range(3)]
-            force = kept_force(r, x, center, e2_ref, mask_ref)
-            for c in range(3):
-                force_ref[c, x] += rotated(force[c], -r)
+            for steps in (REACH[:W], REACH[W:]):
+                force = kept_force(r, steps, x, center, e2_ref, mask_ref)
+                for c in range(3):
+                    force_ref[c, x] += rotated(force[c], -r)
         return carry
 
     results = [
@@ -465,9 +525,9 @@
     def sum_force():
         lax.fori_loop(0, rows, third, 0)
         results[1].start()
-        for ex, src in ((0, disp_ref), (1, new_disp_ref)):
+        for ex in range(2):
             for g in (HIGH, LOW):
-                each(copies(ex, g, src), lambda copy: copy.wait_send())
+                wait_sent(ex, g)
 
     moves = []
     if direct:
@@ -478,7 +538,7 @@
             copy = pltpu.make_async_remote_copy(
                 src_ref=slots.at[me],
                 dst_ref=slots.at[me],
-                send_sem=esend_sem.at[d],
+                send_sem=esend_sem.at[0],
                 recv_sem=erecv_sem.at[0],
                 device_id={
                     "gx": lax.rem(ix + dx, nx),
@@ -488,11 +548,9 @@
                 device_id_type=MESH,
             )
             copy.start()
-            moves.append(copy)
         sum_force()
-        for copy in moves:
-            copy.wait_send()
         landed = slots.at[: nx * ny * nz - 1]
+        pltpu.make_async_copy(landed, landed, esend_sem.at[0]).wait()
         pltpu.make_async_copy(landed, landed, erecv_sem.at[0]).wait()
         value = slots[...]
     else:
@@ -569,7 +627,7 @@
             pltpu.VMEM((depth, width), jnp.float32),
             pltpu.SemaphoreType.DMA((6,)),
             pltpu.SemaphoreType.DMA((2, 2, 7)),
-            pltpu.SemaphoreType.DMA((2, 2, 17)),
+            pltpu.SemaphoreType.DMA((2, 2, 3)),
             pltpu.SemaphoreType.DMA((peers,)),
             pltpu.SemaphoreType.DMA((peers,)),
         ],

time: 36.7 us -> 35.7 us (0.973)
  Pallas kernels: 32.3 us -> 31.4 us
    pallas_call x1, Pallas kernels: 32.3 us -> 31.4 us  [per_device(): pl.pallas_call(functools.partial(step_kernel, counts, depth * counts[2],...]
where the time goes in v4:
time: 35.7 us; the launch traced here: 35.5 us
  Pallas kernels  31.4 us (88%)
  between operations  2.33 us (7%)
  other arithmetic  1.81 us (5%)
    pallas_call x1, Pallas kernels, per_device(): pl.pallas_call(functools.partial(step_kernel, counts, depth * counts[2],...  31.4 us
    add x1, other arithmetic, per_device(): new_velocity = velocity + 0.5 * TIME_STEP * (acc + new_acceleration)  1.81 us

profile of v4, /device:TPU:0, one launch (start us, length us, event | category | flops | bytes accessed | tf_op | source)
XLA Modules:
  0.0 35.5 jit_solution(743340857711185506)
XLA Ops:
  0.6 31.4 %shard_map.75 = (f32[3,8,8,128]{3,2,1,0:T(8,128)}, f32[3,8,8,128]{3,2,1,0:T(8,128)}, f32[1,1]{1,0:T(1,128)}) custom-call(f32[3,8,8,128]{3,2,1,0:T(8,128)} %disp_hbm.1, f32[3,8,8,128]{3,2,1,0:T(8,128)} %vel_hbm.1, f32[3,8,8,128]{3,2,1,0:T(8,128)} %body_hbm.1, s32[12,8,8,128]{3,2,1,0:T(8,128)} %broken_hbm.1), custom_call_target="tpu_custom_call" | custom-call | tf_op jit(solution)/shard_map/pallas_call | solution.py:604
  32.0 1.8 %multiply_add_fusion = (f32[3,8,8,128]{3,2,1,0:T(8,128)}, f32[3,8,8,128]{3,2,1,0:T(8,128)}, f32[3,8,8,128]{3,2,1,0:T(8,128)}) fusion(f32[3,8,8,128]{3,2,1,0:T(8,128)} %vel_hbm.1, f32[3,8,8,128]{3,2,1,0:T(8,128)} %get-tuple-element.7, f32[3,8,8,128]{3,2,1,0:T(8,128)} %get-tuple-element.8, f32[3,8,8,128]{3,2,1,0:T(8,128)} %body_hbm.1, f32[3,8,8,128]{3,2,1,0:T(8,128)} %disp_hbm.1), kind=kLoop, calls=%fused_computation | loop fusion | flops 196608 | bytes 786432 | tf_op jit(solution)/shard_map/add | solution.py:642
